TPU v7x, 256 devices: a whole 4x4x8 slice. The times are simulated.
256 devices in a mesh: g: 256 (over z, y, x, core).
Axes of the slice: x: 4, y: 4, z: 8, core: 2. Of those that a mesh axis runs over, the one named last changes fastest.
Arguments:
- x_store: bfloat16 [524288, 602], P('g')
- frontier_ids: int32 [524288], P('g')
- nbr_one: int32 [131072, 25], P('g')
- nbr_two: int32 [16384, 10], P('g')
- labels: int32 [16384], P('g')
- w_self1: bfloat16 [602, 256], replicated
- w_nbr1: bfloat16 [602, 256], replicated
- w_self2: bfloat16 [256, 41], replicated
- w_nbr2: bfloat16 [256, 41], replicated
Outputs:
- output 1: float32 [], replicated
- output 2: float32 [602, 256], replicated
- output 3: float32 [602, 256], replicated
- output 4: float32 [256, 41], replicated
- output 5: float32 [256, 41], replicated
All inputs are finite; a program needn't handle non-finite values.
Results may differ from a plain program's by a relative error of at most 0.00261.
Values are sent between devices in bfloat16 or wider.
A program may use at most 768 MiB of HBM per device.

v0:
```python
import jax
import jax.numpy as jnp
from jax import lax
from jax.sharding import PartitionSpec as P


def block_pass(x_front, nbr_one, nbr_two, labels, w_self1, w_nbr1, w_self2, w_nbr2, grad_scale):
    seed_count, fan_two = nbr_two.shape
    target_count, fan_one = nbr_one.shape
    hidden, classes = w_self2.shape
    agg_one = (jnp.sum(x_front[nbr_one], axis=1, dtype=jnp.float32) / fan_one).astype(jnp.bfloat16)
    x_target = x_front[:target_count]
    z_one = (jnp.dot(x_target, w_self1, preferred_element_type=jnp.float32)
             + jnp.dot(agg_one, w_nbr1, preferred_element_type=jnp.float32))
    h_one = jnp.maximum(z_one, 0.0).astype(jnp.bfloat16)
    agg_two = (jnp.sum(h_one[nbr_two], axis=1, dtype=jnp.float32) / fan_two).astype(jnp.bfloat16)
    h_seed = h_one[:seed_count]
    logits = (jnp.dot(h_seed, w_self2, preferred_element_type=jnp.float32)
              + jnp.dot(agg_two, w_nbr2, preferred_element_type=jnp.float32))
    log_prob = jax.nn.log_softmax(logits, axis=-1)
    one_hot = (labels[:, None] == jnp.arange(classes, dtype=labels.dtype)[None, :]).astype(jnp.float32)
    loss_sum = -jnp.sum(one_hot * log_prob)
    grad_logits = ((jnp.exp(log_prob) - one_hot) * grad_scale).astype(jnp.bfloat16)
    grad_self2 = jnp.einsum('nh,nc->hc', h_seed, grad_logits, preferred_element_type=jnp.float32)
    grad_nbr2 = jnp.einsum('nh,nc->hc', agg_two, grad_logits, preferred_element_type=jnp.float32)
    grad_seed = jnp.einsum('nc,hc->nh', grad_logits, w_self2, preferred_element_type=jnp.float32)
    grad_agg = jnp.einsum('nc,hc->nh', grad_logits, w_nbr2, preferred_element_type=jnp.float32) / fan_two
    spread = jnp.broadcast_to(grad_agg[:, None, :], (seed_count, fan_two, hidden)).reshape(seed_count * fan_two, hidden)
    row_ids = jnp.concatenate([nbr_two.reshape(-1), jnp.arange(seed_count, dtype=nbr_two.dtype)])
    grad_h = jax.ops.segment_sum(jnp.concatenate([spread, grad_seed], axis=0), row_ids, num_segments=target_count)
    grad_z = jnp.where(z_one > 0, grad_h, 0.0).astype(jnp.bfloat16)
    grad_self1 = jnp.einsum('nf,nh->fh', x_target, grad_z, preferred_element_type=jnp.float32)
    grad_nbr1 = jnp.einsum('nf,nh->fh', agg_one, grad_z, preferred_element_type=jnp.float32)
    return loss_sum, grad_self1, grad_nbr1, grad_self2, grad_nbr2


def solution(mesh):
    group_size = mesh.shape['g']
    to_left = [(source, (source - 1) % group_size) for source in range(group_size)]
    to_right = [(source, (source + 1) % group_size) for source in range(group_size)]

    def device_step(x_local, front_ids, nbr_one, nbr_two, labels, w_self1, w_nbr1, w_self2, w_nbr2):
        my_index = lax.axis_index('g')
        store_rows = x_local.shape[0]
        halo_cap = front_ids.shape[0] // 32
        owner_shard = front_ids // store_rows
        row_offset = front_ids - owner_shard * store_rows
        from_left = owner_shard == (my_index - 1) % group_size
        from_right = owner_shard == (my_index + 1) % group_size
        left_rank = jnp.cumsum(from_left.astype(jnp.int32)) - 1
        right_rank = jnp.cumsum(from_right.astype(jnp.int32)) - 1
        ask_left = jax.ops.segment_sum(jnp.where(from_left, row_offset, 0), jnp.where(from_left, left_rank, halo_cap),
                                       num_segments=halo_cap + 1)[:halo_cap]
        ask_right = jax.ops.segment_sum(jnp.where(from_right, row_offset, 0), jnp.where(from_right, right_rank, halo_cap),
                                        num_segments=halo_cap + 1)[:halo_cap]
        asked_by_right = lax.ppermute(ask_left, 'g', to_left)
        asked_by_left = lax.ppermute(ask_right, 'g', to_right)
        rows_from_left = lax.ppermute(x_local[asked_by_right], 'g', to_right)
        rows_from_right = lax.ppermute(x_local[asked_by_left], 'g', to_left)
        halo_rows = jnp.concatenate([rows_from_left, rows_from_right], axis=0)
        halo_index = jnp.where(from_left, left_rank, halo_cap + right_rank)
        x_front = jnp.where((owner_shard == my_index)[:, None], x_local[row_offset], halo_rows[halo_index])
        grad_scale = 1.0 / (group_size * labels.shape[0])
        loss_sum, grad_self1, grad_nbr1, grad_self2, grad_nbr2 = block_pass(
            x_front, nbr_one, nbr_two, labels, w_self1, w_nbr1, w_self2, w_nbr2, grad_scale)
        mean_loss = lax.psum(loss_sum, 'g') * grad_scale
        grad_sums = lax.psum((grad_self1, grad_nbr1, grad_self2, grad_nbr2), 'g')
        return (mean_loss,) + tuple(grad_sums)

    return jax.shard_map(device_step, mesh=mesh,
                         in_specs=(P('g', None), P('g'), P('g', None), P('g', None), P('g'), P(), P(), P(), P()),
                         out_specs=(P(), P(), P(), P(), P()), check_vma=False)
```

profile of v0, /device:TPU:1, one launch (start us, length us, event | category | flops | bytes accessed | tf_op | source)
XLA Modules:
  0.0 475.1 jit_solution(9631233506121271204)
XLA Ops:
  7.2 0.0 copy-start
  7.2 0.0 all-reduce.5.cloned.1.call-start
  7.3 0.7 broadcast_select_fusion.2
  8.0 0.3 reduce-window.24
  8.3 0.1 slice.48
  8.4 0.1 slice_reduce_fusion
  8.5 0.3 reduce-window.16
  8.8 0.1 slice.46
  8.9 0.1 slice_reduce_fusion.1
  9.0 0.1 fusion.17
  9.1 14.7 %scatter_custom_fusion = s32[65]{0:T(128)S(1)} fusion(s32[2048]{0:T(1024)S(1)} %get-tuple-element.17, s32[2048]{0:T(1024)S(1)} %get-tuple-element.10, s32[]{:T(128)} %constant.68.clone.1), kind=kCustom, calls=%fused_computation.73 | custom fusion | flops 2048 | bytes 264 | tf_op jit(solution)/shard_map/scatter-add | solution.py:52
  23.8 3.3 collective-permute-start
  27.0 14.7 %scatter_custom_fusion.1 = s32[65]{0:T(128)S(1)} fusion(s32[2048]{0:T(1024)S(1)} %get-tuple-element.18, s32[2048]{0:T(1024)S(1)} %get-tuple-element.20, s32[]{:T(128)} %constant.68.clone.1), kind=kCustom, calls=%fused_computation.71 | custom fusion | flops 2048 | bytes 264 | tf_op jit(solution)/shard_map/scatter-add | solution.py:54
  41.7 0.1 collective-permute-start.2
  41.8 0.7 broadcast_compare_fusion.2
  42.5 0.7 compare_select_fusion.1
  43.2 0.8 copy.22
  44.0 0.8 compare_select_fusion
  44.8 0.1 copy.20
  45.0 0.2 reshape.102
  45.2 0.1 copy.21
  45.3 0.1 reshape.110
  45.5 3.1 copy.17
  48.6 0.1 reshape.64
  48.7 9.3 %gather_fusion = bf16[2048,602]{1,0:T(8,128)(2,1)} fusion(bf16[2048,602]{1,0:T(8,128)(2,1)S(1)} %copy.17, s32[2048]{0:T(1024)S(1)} %get-tuple-element.19), kind=kCustom, calls=%fused_computation | custom fusion | bytes 4939776 | tf_op jit(solution)/shard_map/gather | solution.py:62
  58.1 0.0 collective-permute-done
  58.1 0.7 gather_fusion.1
  58.8 0.1 collective-permute-start.1
  58.9 0.0 collective-permute-done.2
  58.9 0.7 gather_fusion.2
  59.6 8.5 %collective-permute-start.3 = (bf16[64,602]{1,0:T(8,128)(2,1)S(1)}, bf16[64,602]{1,0:T(8,128)(2,1)S(1)}, u32[]{:S(2)}, u32[]{:S(2)}) collective-permute-start(bf16[64,602]{1,0:T(8,128)(2,1)S(1)} %gather_fusion.2), channel_id=1, source_target_pairs={{0,255},{1,0},{2,1},{3,2},{4,3},{5,4},{6,5},{7,6},{8,7},{9,8},{10,... | collective-permute-start | bytes 231176 | tf_op jit(solution)/shard_map/ppermute | solution.py:59
  68.2 0.0 collective-permute-done.1
  68.2 0.9 collective-permute-done.3
  69.1 9.3 %gather_fusion.3 = bf16[2048,602]{1,0:T(8,128)(2,1)} fusion(bf16[128,602]{1,0:T(8,128)(2,1)S(1)} %pad_maximum_fusion, s32[2048]{0:T(1024)S(1)} %get-tuple-element.16), kind=kCustom, calls=%fused_computation.3 | custom fusion | bytes 4939776 | tf_op jit(solution)/shard_map/gather | solution.py:62
  78.4 2.8 broadcast_select_fusion
  81.2 37.2 %gather_fusion.4 = bf16[12800,602]{1,0:T(8,128)(2,1)} fusion(bf16[2048,602]{1,0:T(8,128)(2,1)S(1)} %broadcast_select_fusion, s32[13312]{0:T(1024)S(1)} %pad_clamp_fusion), kind=kCustom, calls=%fused_computation.4 | custom fusion | bytes 30873600 | tf_op jit(solution)/shard_map/gather | solution.py:11
  118.4 27.4 %reshape.151 = f32[512,25,602]{2,1,0:T(8,128)} reshape(bf16[12800,602]{1,0:T(8,128)(2,1)} %gather_fusion.4) | data formatting | bytes 46233600 | tf_op jit(solution)/shard_map/convert_element_type | solution.py:11
  145.9 0.0 copy-done.1
  145.9 1.2 fusion.6
  147.0 20.9 %reduce_sum.37 = f32[512,602]{1,0:T(8,128)} reduce(f32[512,25,602]{2,1,0:T(8,128)} %reshape.151, f32[]{:T(128)} %constant.79.clone.1), dimensions={1}, to_apply=%region_6.7 | reduce | flops 7397376 | bytes 32055300 | tf_op jit(solution)/shard_map/reduce_sum | solution.py:11
  167.9 2.6 maximum_convert_fusion
  170.5 2.8 gather_fusion.5
  173.3 0.0 copy-start.3
  173.3 1.1 reshape.152
  174.4 1.4 reduce_sum.38
  175.8 0.0 copy-done.2
  175.8 0.1 fusion.12
  175.9 0.9 fusion.27
  176.9 0.6 multiply_convert_fusion.4
  177.5 0.9 convolution_multiply_fusion
  178.4 0.2 fusion.28
  178.6 1.1 broadcast_in_dim.68
  179.7 2.2 reshape.65
  181.8 7.0 %scatter_custom_fusion.2 = f32[512,256]{1,0:T(8,128)} fusion(s32[704]{0:T(1024)S(1)} %pad_add_fusion, f32[64,256]{1,0:T(8,128)S(1)} %fusion.28, f32[]{:T(128)} %constant.83.clone.1, f32[640,256]{1,0:T(8,128)} %reshape.65, f32[]{:T(128)} %constant.79.clone.1), kind=kCustom, calls=%fused_computation.14 | custom fusion | flops 360448 | bytes 1245192 | tf_op jit(solution)/shard_map/scatter-add | solution.py:30
  188.8 1.3 select_convert_fusion
  190.1 2.5 fusion.9
  192.6 1.2 fusion.4
  193.8 0.0 all-reduce.5.cloned.1.call-update
  193.8 0.1 fusion.10
  193.9 0.1 fusion.14
  194.7 87.8 %all-reduce.6 = (f32[]{:T(128)}, f32[256,41]{0,1:T(8,128)}, f32[256,41]{0,1:T(8,128)}) all-reduce(f32[]{:T(128)S(6)} %neg.3, f32[256,41]{0,1:T(8,128)S(1)} %fusion.10, f32[256,41]{0,1:T(8,128)S(1)} %fusion.14), channel_id=1, replica_groups=mesh['g'=256] {'g'}, use_global_device_ids=true, to_apply=%region_11.12 | all-reduce | flops 20993 | bytes 167944 | tf_op jit(solution)/shard_map/psum | solution.py:66
  283.2 180.0 %all-reduce.5.cloned.1.call-done = (f32[602,256]{1,0:T(8,128)}, f32[602,256]{1,0:T(8,128)}) async-done(((f32[602,256]{1,0:T(8,128)}, f32[602,256]{1,0:T(8,128)}), (f32[602,256]{1,0:T(8,128)}, f32[602,256]{1,0:T(8,128)})) %all-reduce.5.cloned.1.call-update) | async-done | bytes 1232912 | tf_op jit(solution)/shard_map/psum | solution.py:67
  463.2 1.9 copy.28
  465.1 1.9 copy.29
  (18 shorter events, 0.2 us)
Async XLA Ops:
  7.2 160.7 %copy-start = (bf16[602,256]{1,0:T(8,128)(2,1)S(1)}, bf16[602,256]{1,0:T(8,128)(2,1)}, u32[]{:S(2)}) copy-start(bf16[602,256]{1,0:T(8,128)(2,1)} %param.15) | copy-start | bytes 924676
  7.2 456.0 %all-reduce.5.cloned.1.call-start = ((), (), s32[]{:S(2)}) async-start(), calls=%async_computation | async-start | bytes 2490368 | tf_op jit(solution)/shard_map/psum | solution.py:67
  23.8 34.3 %collective-permute-start = (s32[64]{0:T(128)S(1)}, s32[64]{0:T(128)S(1)}, u32[]{:S(2)}, u32[]{:S(2)}) collective-permute-start(s32[64]{0:T(128)S(1)} %bitcast.28), channel_id=1, source_target_pairs={{0,255},{1,0},{2,1},{3,2},{4,3},{5,4},{6,5},{7,6},{8,7},{9,8},{10,... | collective-permute-start | bytes 776 | tf_op jit(solution)/shard_map/ppermute | solution.py:56
  41.7 17.2 %collective-permute-start.2 = (s32[64]{0:T(128)S(1)}, s32[64]{0:T(128)S(1)}, u32[]{:S(2)}, u32[]{:S(2)}) collective-permute-start(s32[64]{0:T(128)S(1)} %bitcast.27), channel_id=1, source_target_pairs={{0,1},{1,2},{2,3},{3,4},{4,5},{5,6},{6,7},{7,8},{8,9},{9,10},{10,1... | collective-permute-start | bytes 776 | tf_op jit(solution)/shard_map/ppermute | solution.py:57
  58.8 9.4 %collective-permute-start.1 = (bf16[64,602]{1,0:T(8,128)(2,1)S(1)}, bf16[64,602]{1,0:T(8,128)(2,1)S(1)}, u32[]{:S(2)}, u32[]{:S(2)}) collective-permute-start(bf16[64,602]{1,0:T(8,128)(2,1)S(1)} %gather_fusion.1), channel_id=1, source_target_pairs={{0,1},{1,2},{2,3},{3,4},{4,5},{5,6},{6,7},{7,8},{8,9},{9,10},{10,1... | collective-permute-start | bytes 231176 | tf_op jit(solution)/shard_map/ppermute | solution.py:58
  59.6 9.4 %collective-permute-start.3 = (bf16[64,602]{1,0:T(8,128)(2,1)S(1)}, bf16[64,602]{1,0:T(8,128)(2,1)S(1)}, u32[]{:S(2)}, u32[]{:S(2)}) collective-permute-start(bf16[64,602]{1,0:T(8,128)(2,1)S(1)} %gather_fusion.2), channel_id=1, source_target_pairs={{0,255},{1,0},{2,1},{3,2},{4,3},{5,4},{6,5},{7,6},{8,7},{9,8},{10,... | collective-permute-start | bytes 231176 | tf_op jit(solution)/shard_map/ppermute | solution.py:59
  118.4 27.4 %copy-start.1 = (bf16[602,256]{1,0:T(8,128)(2,1)S(1)}, bf16[602,256]{1,0:T(8,128)(2,1)}, u32[]{:S(2)}) copy-start(bf16[602,256]{1,0:T(8,128)(2,1)} %param.14) | copy-start | bytes 924676
  170.5 5.3 %copy-start.2 = (bf16[256,41]{0,1:T(8,128)(2,1)S(1)}, bf16[256,41]{0,1:T(8,128)(2,1)}, u32[]{:S(2)}) copy-start(bf16[256,41]{0,1:T(8,128)(2,1)} %param.16) | copy-start | bytes 62980
  173.3 3.6 copy-start.3
Sparse Core Ops, SparseCore 0:
  193.9 269.2 all-reduce.4
where the time goes:
time: 477 us; the launch traced here: 475 us
  waiting for transfers between devices  181 us (38%)
  local copies, waits for them, and re-layouts  101 us (21%)
  blocking collectives  87.8 us (18%)
  other arithmetic  67.1 us (14%)
  between operations  16.7 us (4%)
  starting transfers between devices  12 us (3%)
  matrix products  9.85 us (2%)
    psum x1, waiting for transfers between devices, device_step(): grad_sums = lax.psum((grad_self1, grad_nbr1, grad_self2, grad_nbr2), 'g')  180 us
    psum x1, blocking collectives, device_step(): mean_loss = lax.psum(loss_sum, 'g') * grad_scale  87.8 us
    gather x1, local copies, waits for them, and re-layouts, block_pass(): x_front[nbr_one]  37.2 us
    convert_element_type x1, local copies, waits for them, and re-layouts, block_pass(): jnp.sum(x_front[nbr_one], axis=1, dtype=jnp.float32) / fan_one  27.4 us
    reduce_sum x1, other arithmetic, block_pass(): jnp.sum(x_front[nbr_one], axis=1, dtype=jnp.float32) / fan_one  20.9 us
    scatter-add x1, other arithmetic, device_step(): jax.ops.segment_sum(jnp.where(from_left, row_offset, 0), jnp.where(from_l...  14.7 us
    scatter-add x1, other arithmetic, device_step(): jax.ops.segment_sum(jnp.where(from_right, row_offset, 0), jnp.where(from_...  14.7 us
  transfers between devices with their start and end apart: 5, of which 2 were waited for; matrix products, arithmetic and copies ran while one was open for 7% of the time, Pallas kernels for 0%

commit v1 on v0

v1 whole, which is shorter than its diff:
```python
import functools

import jax
import jax.numpy as jnp
from jax import lax
from jax.experimental import pallas as pl
from jax.experimental.pallas import tpu as pltpu
from jax.sharding import PartitionSpec as P

MESH = pl.DeviceIdType.MESH
F32, BF16, I32 = jnp.float32, jnp.bfloat16, jnp.int32
VMEM = pltpu.VMEM

HALO = 64
FIELDS, FIELD_BITS = 6, 5
CHUNK_A, CHUNK_B = 6, 5


def dims_of(group):
    return {256: (4, 4, 8), 16: (2, 2, 2)}[group]


def dot(a, b, ca=1, cb=0):
    return lax.dot_general(a, b, (((ca,), (cb,)), ((), ())), preferred_element_type=F32)


def iota(shape, dim):
    return lax.broadcasted_iota(I32, shape, dim)


def frontier_ext(fid, me, group, rows_log2):
    store = 1 << rows_log2
    owner = lax.shift_right_logical(fid, rows_log2)
    off = lax.bitwise_and(fid, store - 1)
    left, right = lax.rem(me + group - 1, group), lax.rem(me + 1, group)
    is_l, is_r = owner == left, owner == right
    mask = jnp.concatenate([jnp.where(is_l, 1.0, 0.0), jnp.where(is_r, 1.0, 0.0)], axis=0).astype(BF16)
    n = fid.shape[0]
    upper = jnp.where(iota((128, 128), 0) < iota((128, 128), 1), 1.0, 0.0).astype(BF16)
    ri, ci = iota((2 * n, 2 * n), 0), iota((2 * n, 2 * n), 1)
    before = jnp.where((ci < ri) & ((ci < n) == (ri < n)), 1.0, 0.0).astype(BF16)
    ones = jnp.ones((128, 128), BF16)
    rank = dot(mask, upper) + dot(dot(before, mask).astype(BF16), ones)
    rank = rank.astype(I32)
    rank_l, rank_r = rank[:n], rank[n:]
    ext = jnp.where(is_l, store + rank_l, jnp.where(is_r, store + HALO + rank_r, off))
    return ext, off


def lanes_of(a):
    return jnp.concatenate([a[i:i + 1, :] for i in range(a.shape[0])], axis=1)


def ask_rows(ext, off, store):
    key = lanes_of(ext) - store
    offs = lanes_of(off)
    pick = jnp.where(iota((2 * HALO, key.shape[1]), 0) == key, 1.0, 0.0).astype(BF16)
    row = iota((16, key.shape[1]), 0)
    hi, lo = lax.shift_right_logical(offs, 6), lax.bitwise_and(offs, 63)
    parts = jnp.where(row == 0, hi, jnp.where(row == 1, lo, 0)).astype(F32).astype(BF16)
    got = dot(parts, pick, 1, 1).astype(I32)
    return got[0:1] * 64 + got[1:2]


def halo_kernel(group, fid_ref, x_ref, halo_ref, ext_ref, ask, ask_in, rep, rep_in, send, recv):
    me = lax.axis_index('g')
    left, right = lax.rem(me + group - 1, group), lax.rem(me + 1, group)
    barrier = pltpu.get_barrier_semaphore()
    for nb in (left, right):
        pl.semaphore_signal(barrier, inc=1, device_id=(nb,), device_id_type=MESH)
    feat, store = x_ref.shape
    half = rep.shape[1]
    ext, off = frontier_ext(fid_ref[...], me, group, store.bit_length() - 1)
    ext_ref[...] = ext
    ask[...] = jnp.broadcast_to(ask_rows(ext, off, store), ask.shape)
    pl.semaphore_wait(barrier, 2)
    asks = []
    for i, nb in enumerate((left, right)):
        asks.append(pltpu.make_async_remote_copy(ask, ask_in.at[i], send.at[i], recv.at[i], device_id=(nb,), device_id_type=MESH))
        asks[-1].start()
    for cp in asks:
        cp.wait_recv()
    lane = iota((1, 128), 1)
    want = jnp.where(lane < HALO, ask_in[0, 0:1, :], ask_in[1, 0:1, :])
    pick = jnp.where(iota((store, 128), 0) == want, 1.0, 0.0).astype(BF16)
    out = dot(x_ref[...], pick)
    pad = 2 * half - feat
    top = out[0:half]
    bot = jnp.concatenate([out[half:feat], jnp.zeros((pad, 128), F32)], axis=0)
    lo = iota((half, 128), 1) < HALO
    rep[0] = jnp.where(lo, top, pltpu.roll(bot, HALO, 1)).astype(BF16)
    rep[1] = jnp.where(lo, pltpu.roll(top, HALO, 1), bot).astype(BF16)
    reps = []
    for i, nb in enumerate((right, left)):
        reps.append(pltpu.make_async_remote_copy(rep.at[i], rep_in.at[i], send.at[2 + i], recv.at[2 + i], device_id=(nb,), device_id_type=MESH))
        reps[-1].start()
    for cp in reps:
        cp.wait_recv()
    from_l, from_r = rep_in[0].astype(F32), rep_in[1].astype(F32)
    halo_ref[0:half, :] = jnp.where(lo, from_l, pltpu.roll(from_r, HALO, 1)).astype(BF16)
    halo_ref[half:2 * half, :] = jnp.where(lo, pltpu.roll(from_l, HALO, 1), from_r).astype(BF16)
    for cp in asks + reps:
        cp.wait_send()


def local_kernel(scale, feat, classes, seeds, fan_one, fan_two,
                 x_ref, halo_ref, ext_ref, n1_ref, n2_ref, lab_ref, ws1_ref, wn1_ref, ws2_ref, wn2_ref,
                 g_ref, idx, acc, nf, z_ref):
    store = x_ref.shape[1]
    targets = n1_ref.shape[1]
    width = acc.shape[0]
    table = ext_ref[...]
    for r0 in range(0, n1_ref.shape[0], 8):
        for c0 in range(0, targets, 128):
            pos = n1_ref[r0:r0 + 8, c0:c0 + 128]
            hi = lax.shift_right_logical(pos, 7)
            lo = lax.bitwise_and(pos, 127)
            val = jnp.zeros((8, 128), I32)
            for h in range(table.shape[0]):
                row = jnp.broadcast_to(table[h:h + 1, :], (8, 128))
                val = jnp.where(hi == h, jnp.take_along_axis(row, lo, axis=1, mode='promise_in_bounds'), val)
            fld = jnp.zeros((8, 128), I32)
            for f in range(1, FIELDS):
                fld = fld + jnp.where(val >= f * width, 1, 0)
            idx[0, r0:r0 + 8, c0:c0 + 128] = val - fld * width
            idx[1, r0:r0 + 8, c0:c0 + 128] = lax.shift_left(jnp.ones((8, 128), I32), fld * FIELD_BITS)
    block = 16

    def count_block(b, carry):
        base = pl.multiple_of(b * block, block)
        for c0 in range(0, targets, 256):
            row = iota((block, 256), 0) + base
            tot = jnp.zeros((block, 256), I32)
            for k in range(fan_one):
                tot = tot + jnp.where(row == idx[0, k:k + 1, c0:c0 + 256], idx[1, k:k + 1, c0:c0 + 256], 0)
            acc[pl.ds(base, block), c0:c0 + 256] = tot
        return carry

    lax.fori_loop(0, width // block, count_block, 0)
    for f in range(FIELDS):
        part = lax.bitwise_and(lax.shift_right_logical(acc[...], f * FIELD_BITS), (1 << FIELD_BITS) - 1)
        nf[f * width:(f + 1) * width, targets:2 * targets] = part.astype(F32).astype(BF16)
    first = lanes_of(ext_ref[0:targets // 128, :])
    nf[:, 0:targets] = jnp.where(iota((nf.shape[0], targets), 0) == first, 1.0, 0.0).astype(BF16)

    halo = halo_ref[...]
    both = dot(x_ref[...], nf[0:store, :]) + dot(halo[0:feat], nf[store:store + 2 * HALO, :])
    x_t = both[:, 0:targets].astype(BF16)
    a_t = (both[:, targets:] * (1.0 / fan_one)).astype(BF16)
    z = dot(ws1_ref[...], x_t, 0, 0) + dot(wn1_ref[...], a_t, 0, 0)
    z_ref[...] = z
    h = jnp.maximum(z, 0.0).astype(BF16)
    lane = iota((1, 128), 1)
    m2 = jnp.zeros((targets, 128), F32)
    for k in range(fan_two):
        pos = jnp.where(lane < seeds, n2_ref[k:k + 1, :], -1)
        m2 = m2 + jnp.where(iota((targets, 128), 0) == pos, 1.0, 0.0)
    m2 = m2.astype(BF16)
    a2 = (dot(h, m2) * (1.0 / fan_two)).astype(BF16)
    hs = h[:, 0:128]
    cpad = ws2_ref.shape[0]
    crow = iota((cpad, 128), 0)
    wok = iota((cpad, 1), 0) < classes
    ws2 = jnp.where(wok, ws2_ref[...].astype(F32), 0.0).astype(BF16)
    wn2 = jnp.where(wok, wn2_ref[...].astype(F32), 0.0).astype(BF16)
    logits = dot(ws2, hs) + dot(wn2, a2)
    logits = jnp.where(crow < classes, logits, -1e30)
    top = jnp.max(logits, axis=0, keepdims=True)
    shifted = logits - top
    log_prob = shifted - jnp.log(jnp.sum(jnp.exp(shifted), axis=0, keepdims=True))
    label = jnp.where(lane < seeds, lab_ref[...], -1)
    hit = crow == label
    loss = -jnp.sum(jnp.where(hit, log_prob, 0.0))
    g = (jnp.exp(log_prob) - jnp.where(hit, 1.0, 0.0)) * scale
    g = jnp.where((crow < classes) & (lane < seeds), g, 0.0).astype(BF16)
    d_s2 = dot(g, hs, 1, 1)
    d_n2 = dot(g, a2, 1, 1)
    lrow = iota(d_s2.shape, 0) == classes
    d_s2 = jnp.where(lrow, loss, d_s2)
    g_seed = dot(ws2, g, 0, 0)
    g_agg = dot(wn2, g, 0, 0) * (1.0 / fan_two)
    p0 = g_agg.astype(BF16)
    r1 = g_agg - p0.astype(F32)
    p1 = r1.astype(BF16)
    p2 = (r1 - p1.astype(F32)).astype(BF16)
    d_h = dot(p0, m2, 1, 1) + (dot(p1, m2, 1, 1) + dot(p2, m2, 1, 1))
    d_h = d_h + jnp.concatenate([g_seed, jnp.zeros((g_seed.shape[0], targets - 128), F32)], axis=1)
    d_z = jnp.where(z_ref[...] > 0, d_h, 0.0).astype(BF16)
    tail = jnp.zeros((halo.shape[0] - feat, d_z.shape[0]), F32)
    at = 0
    for mat in (jnp.concatenate([dot(x_t, d_z, 1, 1), tail], axis=0),
                jnp.concatenate([dot(a_t, d_z, 1, 1), tail], axis=0), d_s2, d_n2):
        n = mat.shape[0] // 8
        for c0 in range(0, mat.shape[1], 128):
            g_ref[at:at + n] = mat[:, c0:c0 + 128].reshape(n, 8, 128)
            at += n
    g_ref[at:] = jnp.zeros((g_ref.shape[0] - at, 8, 128), F32)


def reduce_kernel(group, g_ref, r_ref, rc, part, l1a, l1b, w2a, w2b, l2a, l2b, zc, lz, zg, full, send, recv):
    nx, ny, nz = dims_of(group)
    ca, cb = CHUNK_A, CHUNK_B
    cx, cy, zn = ny * ca, nx * cb, ca + cb
    zsize = -(-zn // nz)
    off_b = nx * cx
    half = off_b + ny * cy
    me = lax.axis_index('g')
    core = lax.rem(me, 2)
    mx = lax.rem(me // 2, nx)
    my = lax.rem(me // (2 * nx), ny)
    mz = me // (2 * nx * ny)

    def dev(z, y, x, c):
        return ((z * ny + y) * nx + x) * 2 + c

    mate = dev(mz, my, mx, 1 - core)
    xs = [lax.rem(mx + d, nx) for d in range(nx)]
    ys = [lax.rem(my + d, ny) for d in range(ny)]
    zs = [lax.rem(mz + d, nz) for d in range(nz)]
    xdev = [dev(mz, my, x, core) for x in xs]
    ydev = [dev(mz, y, mx, core) for y in ys]
    zdev = [dev(z, my, mx, core) for z in zs]

    barrier = pltpu.get_barrier_semaphore()
    peers = [mate] + xdev[1:] + ydev[1:] + zdev[1:]
    for nb in peers:
        pl.semaphore_signal(barrier, inc=1, device_id=(nb,), device_id_type=MESH)
    pl.semaphore_wait(barrier, len(peers))

    copies = []

    def put(src, dst, to):
        k = len(copies)
        cp = pltpu.make_async_remote_copy(src, dst, send.at[k], recv.at[k], device_id=(to,), device_id_type=MESH)
        cp.start()
        copies.append(cp)
        return cp

    pieces = []
    for i in range(max(nx, ny)):
        if i < nx:
            d = (i + 1) % nx
            pieces.append((0, d, xs[d] * cx, cx))
        if i < ny:
            d = (i + 1) % ny
            pieces.append((1, d, off_b + ys[d] * cy, cy))
    other, mine = (1 - core) * half, core * half
    arrive = [put(g_ref.at[pl.ds(other + o, n)], rc.at[pl.ds(o, n)], mate) for _, _, o, n in pieces]
    in_a, in_b = [], []
    for (kind, d, o, n), cp in zip(pieces, arrive):
        cp.wait_recv()
        part[pl.ds(o, n)] = g_ref[pl.ds(mine + o, n)] + rc[pl.ds(o, n)]
        if d:
            if kind == 0:
                in_a.append((put(part.at[pl.ds(o, n)], l1a.at[d - 1], xdev[d]), d - 1))
            else:
                in_b.append((put(part.at[pl.ds(o, n)], l1b.at[d - 1], ydev[d]), d - 1))
    tot = part[pl.ds(mx * cx, cx)]
    for cp, s in in_a:
        cp.wait_recv()
        tot = tot + l1a[s]
    w2a[...] = tot
    in_a = [(put(w2a.at[pl.ds(ys[d] * ca, ca)], l2a.at[d - 1], ydev[d]), d - 1) for d in range(1, ny)]
    tot = part[pl.ds(off_b + my * cy, cy)]
    for cp, s in in_b:
        cp.wait_recv()
        tot = tot + l1b[s]
    w2b[...] = tot
    in_b = [(put(w2b.at[pl.ds(xs[d] * cb, cb)], l2b.at[d - 1], xdev[d]), d - 1) for d in range(1, nx)]
    tot = w2a[pl.ds(my * ca, ca)]
    for cp, s in in_a:
        cp.wait_recv()
        tot = tot + l2a[s]
    zc[0:ca] = tot
    tot = w2b[pl.ds(mx * cb, cb)]
    for cp, s in in_b:
        cp.wait_recv()
        tot = tot + l2b[s]
    zc[ca:zn] = tot
    in_z = [put(zc.at[pl.ds((zn * zs[d]) // nz, zsize)], lz.at[d - 1], zdev[d]) for d in range(1, nz)]
    tot = zc[pl.ds((zn * mz) // nz, zsize)]
    for s, cp in enumerate(in_z):
        cp.wait_recv()
        tot = tot + lz[s]
    zg[mz] = tot
    in_z = [put(zg.at[mz], zg.at[mz], zdev[d]) for d in range(1, nz)]
    for cp in in_z:
        cp.wait_recv()
    at_a = mine + mx * cx + my * ca
    at_b = mine + off_b + my * cy + mx * cb
    for z in range(nz):
        lo = (zn * z) // nz
        end = (zn * (z + 1)) // nz if z + 1 < nz else zn
        for t in range(lo, end):
            at = at_a + t if t < ca else at_b + (t - ca)
            full[pl.ds(at, 1)] = zg[z, t - lo:t - lo + 1]
    in_a = [put(full.at[pl.ds(at_a, ca)], full.at[pl.ds(at_a, ca)], ydev[d]) for d in range(1, ny)]
    in_b = [put(full.at[pl.ds(at_b, cb)], full.at[pl.ds(at_b, cb)], xdev[d]) for d in range(1, nx)]
    row_a, row_b = mine + mx * cx, mine + off_b + my * cy
    for cp in in_a:
        cp.wait_recv()
    in_a = [put(full.at[pl.ds(row_a, cx)], full.at[pl.ds(row_a, cx)], xdev[d]) for d in range(1, nx)]
    for cp in in_b:
        cp.wait_recv()
    in_b = [put(full.at[pl.ds(row_b, cy)], full.at[pl.ds(row_b, cy)], ydev[d]) for d in range(1, ny)]
    back = [put(full.at[pl.ds(row_a, cx)], full.at[pl.ds(row_a, cx)], mate),
            put(full.at[pl.ds(row_b, cy)], full.at[pl.ds(row_b, cy)], mate)]
    for i in range(max(nx, ny) - 1):
        if i < nx - 1:
            in_a[i].wait_recv()
            at = mine + lax.rem(mx + nx - 1 - i, nx) * cx
            back.append(put(full.at[pl.ds(at, cx)], full.at[pl.ds(at, cx)], mate))
        if i < ny - 1:
            in_b[i].wait_recv()
            at = mine + off_b + lax.rem(my + ny - 1 - i, ny) * cy
            back.append(put(full.at[pl.ds(at, cy)], full.at[pl.ds(at, cy)], mate))
    for cp in back:
        cp.wait_recv()
    for cp in copies:
        cp.wait_send()
    r_ref[...] = full[...]


def copy_count(group):
    nx, ny, nz = dims_of(group)
    return 2 * (nx + ny) + 4 * (nx - 1 + ny - 1) + 2 * (nz - 1)


def reduce_call(group, tiles):
    nx, ny, nz = dims_of(group)
    ca, cb = CHUNK_A, CHUNK_B
    cx, cy, zn = ny * ca, nx * cb, ca + cb
    zsize = -(-zn // nz)
    half = nx * cx + ny * cy
    total = 2 * half
    n = copy_count(group)

    def buf(*lead):
        return VMEM((*lead, 8, 128), F32)

    return pl.pallas_call(
        functools.partial(reduce_kernel, group),
        name='gradient_sum',
        out_shape=jax.ShapeDtypeStruct((total, 8, 128), F32),
        in_specs=[pl.BlockSpec(memory_space=VMEM)],
        out_specs=pl.BlockSpec(memory_space=VMEM),
        scratch_shapes=[buf(half), buf(half), buf(nx - 1, cx), buf(ny - 1, cy), buf(cx), buf(cy),
                        buf(ny - 1, ca), buf(nx - 1, cb), buf(zn), buf(nz - 1, zsize), buf(nz, zsize), buf(total),
                        pltpu.SemaphoreType.DMA((n,)), pltpu.SemaphoreType.DMA((n,))],
        compiler_params=pltpu.CompilerParams(collective_id=1, has_side_effects=True),
    )(tiles)


def output_kernel(scale, r_ref, loss_ref, s1_ref, n1_ref, s2_ref, n2_ref):
    at = 0
    classes = s2_ref.shape[0]
    for ref in (s1_ref, n1_ref, s2_ref, n2_ref):
        rows, cols = ref.shape
        n = -(-rows // 8)
        for c0 in range(0, cols, 128):
            val = r_ref[at:at + n].reshape(n * 8, 128)
            ref[:, c0:c0 + 128] = val[0:rows]
            if ref is s2_ref and c0 == 0:
                loss_ref[...] = val[classes:classes + 1, 0:1] * scale
            at += n


def solution(mesh):
    group = mesh.shape['g']

    def device_step(x_local, front_ids, nbr_one, nbr_two, labels, w_self1, w_nbr1, w_self2, w_nbr2):
        store, feat = x_local.shape
        targets, fan_one = nbr_one.shape
        seeds, fan_two = nbr_two.shape
        hidden, classes = w_self2.shape
        frows = -(-feat // 32) * 32
        scale = 1.0 / (group * seeds)
        x_t = x_local.T
        fid = front_ids.reshape(-1, 128)
        vm = pl.BlockSpec(memory_space=VMEM)
        halo, ext = pl.pallas_call(
            functools.partial(halo_kernel, group),
            name='halo_rows',
            out_shape=[jax.ShapeDtypeStruct((frows, 2 * HALO), BF16), jax.ShapeDtypeStruct(fid.shape, I32)],
            in_specs=[vm, vm], out_specs=[vm, vm],
            scratch_shapes=[VMEM((8, 128), I32), VMEM((2, 8, 128), I32), VMEM((2, frows // 2, 128), BF16),
                            VMEM((2, frows // 2, 128), BF16), pltpu.SemaphoreType.DMA((4,)), pltpu.SemaphoreType.DMA((4,))],
            compiler_params=pltpu.CompilerParams(collective_id=0, has_side_effects=True),
        )(fid, x_t)
        width = -(-(store + 2 * HALO) // (FIELDS * 16)) * 16
        nx, ny, nz = dims_of(group)
        tiles = 2 * nx * ny * (CHUNK_A + CHUNK_B)
        tiles = max(tiles, 352)
        kpad, cpad = -(-fan_one // 8) * 8, -(-classes // 16) * 16

        def full(*shape):
            return pl.BlockSpec(shape, lambda i: (0,) * len(shape))

        grads = pl.pallas_call(
            functools.partial(local_kernel, scale, feat, classes, seeds, fan_one, fan_two),
            name='local_step',
            grid=(1,),
            out_shape=jax.ShapeDtypeStruct((tiles, 8, 128), F32),
            in_specs=[full(feat, store), full(frows, 2 * HALO), full(*fid.shape), full(kpad, targets), full(16, 128),
                      full(1, 128), full(feat, hidden), full(feat, hidden), full(cpad, hidden), full(cpad, hidden)],
            out_specs=full(tiles, 8, 128),
            scratch_shapes=[VMEM((2, kpad, targets), I32), VMEM((width, targets), I32),
                            VMEM((FIELDS * width, 2 * targets), BF16), VMEM((hidden, targets), F32)],
            compiler_params=pltpu.CompilerParams(vmem_limit_bytes=60 * 1024 * 1024),
        )(x_t, halo, ext, nbr_one.T, nbr_two.T, labels.reshape(1, -1), w_self1, w_nbr1, w_self2.T, w_nbr2.T)
        if group == 256:
            sums = reduce_call(group, grads)
        else:
            step = 2 * nx * ny * (CHUNK_A + CHUNK_B)
            sums = jnp.concatenate([reduce_call(group, grads[i:i + step]) for i in range(0, tiles, step)])
        loss, d_s1, d_n1, d_s2, d_n2 = pl.pallas_call(
            functools.partial(output_kernel, scale),
            name='split_outputs',
            out_shape=[jax.ShapeDtypeStruct((1, 1), F32), jax.ShapeDtypeStruct((feat, hidden), F32),
                       jax.ShapeDtypeStruct((feat, hidden), F32), jax.ShapeDtypeStruct((classes, hidden), F32),
                       jax.ShapeDtypeStruct((classes, hidden), F32)],
            in_specs=[vm], out_specs=[vm] * 5,
        )(sums)
        return loss[0, 0], d_s1, d_n1, d_s2.T, d_n2.T

    return jax.shard_map(device_step, mesh=mesh,
                         in_specs=(P('g', None), P('g'), P('g', None), P('g', None), P('g'), P(), P(), P(), P()),
                         out_specs=(P(), P(), P(), P(), P()), check_vma=False)
```

time: 477 us -> 76.3 us (0.16)
  waiting for transfers between devices: 181 us -> 0 us
  local copies, waits for them, and re-layouts: 101 us -> 0 us
  blocking collectives: 87.8 us -> 0 us
  Pallas kernels: 0 us -> 75.5 us
  other arithmetic: 67.1 us -> 0 us
  between operations: 16.7 us -> 0.65 us
  starting transfers between devices: 12 us -> 0 us
  matrix products: 9.85 us -> 0 us
    psum x1 -> x0, waiting for transfers between devices: 180 us -> none  [device_step(): grad_sums = lax.psum((grad_self1, grad_nbr1, grad_self2, grad_nbr2), 'g')]
    psum x1 -> x0, blocking collectives: 87.8 us -> none  [device_step(): mean_loss = lax.psum(loss_sum, 'g') * grad_scale]
    pallas_call x0 -> x4, Pallas kernels: none -> 75.5 us  [the longest x1 44.7 us: reduce_call(): pl.pallas_call(functools.partial(reduce_kernel, group), name='gradient_su...]
    gather x6 -> x0, local copies, waits for them, and re-layouts: 60.1 us -> none  [the longest x1 37.2 us: block_pass(): x_front[nbr_one]]
    scatter-add x3 -> x0, other arithmetic: 36.3 us -> none  [the longest x1 14.7 us: device_step(): jax.ops.segment_sum(jnp.where(from_left, row_offset, 0), jnp.where(from_l...]
    convert_element_type x2 -> x0, local copies, waits for them, and re-layouts: 28.5 us -> none  [the longest x1 27.4 us: block_pass(): jnp.sum(x_front[nbr_one], axis=1, dtype=jnp.float32) / fan_one]
    reduce_sum x3 -> x0, other arithmetic: 22.3 us -> none  [the longest x1 20.9 us: block_pass(): jnp.sum(x_front[nbr_one], axis=1, dtype=jnp.float32) / fan_one]
    ppermute x4 -> x0, starting transfers between devices: 11.9 us -> none  [the longest x1 8.52 us: device_step(): rows_from_right = lax.ppermute(x_local[asked_by_left], 'g', to_left)]
  transfers between devices with their start and end apart: 5 -> 0, of which waited for: 2 -> 0; matrix products, arithmetic and copies ran while one was open for 7% -> 0% of each run, Pallas kernels for 0% -> 0%
where the time goes in v1:
time: 76.3 us; the launch traced here: 76.1 us
  Pallas kernels  75.5 us (99%)
    pallas_call x1, Pallas kernels, reduce_call(): pl.pallas_call(functools.partial(reduce_kernel, group), name='gradient_su...  44.7 us
    pallas_call x1, Pallas kernels, device_step(): pl.pallas_call(functools.partial(halo_kernel, group), name='halo_rows', o...  17.7 us
    pallas_call x1, Pallas kernels, device_step(): pl.pallas_call(functools.partial(local_kernel, scale, feat, classes, seed...  10.6 us
    pallas_call x1, Pallas kernels, device_step(): pl.pallas_call(functools.partial(output_kernel, scale), name='split_outpu...  2.46 us

profile of v1, /device:TPU:1, one launch (start us, length us, event | category | flops | bytes accessed | tf_op | source)
XLA Modules:
  0.0 76.1 jit_solution(1348545618721691437)
XLA Ops:
  0.6 17.7 %halo_rows.1 = (bf16[608,128]{1,0:T(8,128)(2,1)}, s32[16,128]{1,0:T(8,128)}) custom-call(s32[16,128]{1,0:T(8,128)} %bitcast.15, bf16[602,2048]{1,0:T(8,128)(2,1)} %bitcast.10), custom_call_target="tpu_custom_call" | custom-call | tf_op jit(solution)/shard_map/halo_rows/pallas_call | solution.py:381
  18.4 10.6 %local_step.1.g_ref = f32[352,8,128]{2,1,0:T(8,128)} custom-call(bf16[602,2048]{1,0:T(8,128)(2,1)} %bitcast.11, bf16[608,128]{1,0:T(8,128)(2,1)} %get-tuple-element.12.halo_ref, s32[16,128]{1,0:T(8,128)} %get-tuple-element.13.ext_ref, s32[25,512]{1,0:T(8,128)} %bitcast.12, s32[10,64]{1,0:T(8,128)} %bitcast.16, s32[1,64]{1,0:T(1,128)} %bitcast.17, ...), custom_call_target="tpu_custom_call" | custom-call | tf_op jit(solution)/shard_map/local_step/pallas_call | solution.py:399
  29.0 44.7 %gradient_sum.1.r_ref = f32[352,8,128]{2,1,0:T(8,128)} custom-call(f32[352,8,128]{2,1,0:T(8,128)} %local_step.1.g_ref), custom_call_target="tpu_custom_call" | custom-call | tf_op jit(solution)/shard_map/gradient_sum/pallas_call | solution.py:341
  73.6 2.5 %split_outputs.1 = (f32[1,1]{1,0:T(1,128)}, f32[602,256]{1,0:T(8,128)}, f32[602,256]{1,0:T(8,128)}, f32[41,256]{1,0:T(8,128)}, f32[41,256]{1,0:T(8,128)}) custom-call(f32[352,8,128]{2,1,0:T(8,128)} %gradient_sum.1.r_ref), custom_call_target="tpu_custom_call" | custom-call | tf_op jit(solution)/shard_map/split_outputs/pallas_call | solution.py:416

commit v2 on v1

v2 whole, which is shorter than its diff:
```python
import functools

import jax
import jax.numpy as jnp
from jax import lax
from jax.experimental import pallas as pl
from jax.experimental.pallas import tpu as pltpu
from jax.sharding import PartitionSpec as P

MESH = pl.DeviceIdType.MESH
F32, BF16, I32 = jnp.float32, jnp.bfloat16, jnp.int32
VMEM = pltpu.VMEM

HALO = 64
FIELDS, FIELD_BITS = 6, 5


def dims_of(group):
    return {256: (4, 4, 8), 16: (2, 2, 2)}[group]


def chunks_of(group):
    return {256: (6, 5), 16: (21, 20)}[group]


def dot(a, b, ca=1, cb=0):
    return lax.dot_general(a, b, (((ca,), (cb,)), ((), ())), preferred_element_type=F32)


def iota(shape, dim):
    return lax.broadcasted_iota(I32, shape, dim)


def frontier_ext(fid, me, group, rows_log2):
    store = 1 << rows_log2
    owner = lax.shift_right_logical(fid, rows_log2)
    off = lax.bitwise_and(fid, store - 1)
    left, right = lax.rem(me + group - 1, group), lax.rem(me + 1, group)
    is_l, is_r = owner == left, owner == right
    mask = jnp.concatenate([jnp.where(is_l, 1.0, 0.0), jnp.where(is_r, 1.0, 0.0)], axis=0).astype(BF16)
    n = fid.shape[0]
    upper = jnp.where(iota((128, 128), 0) < iota((128, 128), 1), 1.0, 0.0).astype(BF16)
    ri, ci = iota((2 * n, 2 * n), 0), iota((2 * n, 2 * n), 1)
    before = jnp.where((ci < ri) & ((ci < n) == (ri < n)), 1.0, 0.0).astype(BF16)
    ones = jnp.ones((128, 128), BF16)
    rank = dot(mask, upper) + dot(dot(before, mask).astype(BF16), ones)
    rank = rank.astype(I32)
    rank_l, rank_r = rank[:n], rank[n:]
    ext = jnp.where(is_l, store + rank_l, jnp.where(is_r, store + HALO + rank_r, off))
    return ext, off


def lanes_of(a):
    return jnp.concatenate([a[i:i + 1, :] for i in range(a.shape[0])], axis=1)


def ask_rows(ext, off, store):
    key = lanes_of(ext) - store
    offs = lanes_of(off)
    pick = jnp.where(iota((2 * HALO, key.shape[1]), 0) == key, 1.0, 0.0).astype(BF16)
    row = iota((16, key.shape[1]), 0)
    hi, lo = lax.shift_right_logical(offs, 6), lax.bitwise_and(offs, 63)
    parts = jnp.where(row == 0, hi, jnp.where(row == 1, lo, 0)).astype(F32).astype(BF16)
    got = dot(parts, pick, 1, 1).astype(I32)
    return got[0:1] * 64 + got[1:2]


def step_kernel(group, scale, fid_ref, x_hbm, n1_ref, n2_ref, lab_ref, ws1_hbm, wn1_hbm, ws2_ref, wn2_ref, r_ref,
                x_ref, ws1_ref, wn1_ref, in_sem, ask, ask_in, rep, rep_in, hsend, hrecv,
                small, idx, acc, nf, both, z_ref, gpad, g,
                rc, part, l1a, l1b, w2a, w2b, l2a, l2b, zc, lz, zg, full, send, recv):
    nx, ny, nz = dims_of(group)
    ca, cb = chunks_of(group)
    cx, cy, zn = ny * ca, nx * cb, ca + cb
    zsize = -(-zn // nz)
    off_b = nx * cx
    half = off_b + ny * cy
    me = lax.axis_index('g')
    core = lax.rem(me, 2)
    mx = lax.rem(me // 2, nx)
    my = lax.rem(me // (2 * nx), ny)
    mz = me // (2 * nx * ny)

    def dev(z, y, x, c):
        return ((z * ny + y) * nx + x) * 2 + c

    mate = dev(mz, my, mx, 1 - core)
    xs = [lax.rem(mx + d, nx) for d in range(nx)]
    ys = [lax.rem(my + d, ny) for d in range(ny)]
    zs = [lax.rem(mz + d, nz) for d in range(nz)]
    xdev = [dev(mz, my, x, core) for x in xs]
    ydev = [dev(mz, y, mx, core) for y in ys]
    zdev = [dev(z, my, mx, core) for z in zs]
    left, right = lax.rem(me + group - 1, group), lax.rem(me + 1, group)

    barrier = pltpu.get_barrier_semaphore()
    peers = [left, right, mate] + xdev[1:] + ydev[1:] + zdev[1:]
    for nb in peers:
        pl.semaphore_signal(barrier, inc=1, device_id=(nb,), device_id_type=MESH)
    loads = [pltpu.make_async_copy(s, d, in_sem.at[i]) for i, (s, d) in
             enumerate(((x_hbm, x_ref), (ws1_hbm, ws1_ref), (wn1_hbm, wn1_ref)))]
    for cp in loads:
        cp.start()

    feat, store = x_ref.shape
    targets = n1_ref.shape[1]
    fan_one = n1_ref.shape[0]
    fan_two, seeds = n2_ref.shape
    classes = ws2_ref.shape[0]
    width = acc.shape[0]
    hrows = rep.shape[1]
    ext, off = frontier_ext(fid_ref[...], me, group, store.bit_length() - 1)
    ask[...] = jnp.broadcast_to(ask_rows(ext, off, store), ask.shape)
    pl.semaphore_wait(barrier, len(peers))
    asks = []
    for i, nb in enumerate((left, right)):
        asks.append(pltpu.make_async_remote_copy(ask, ask_in.at[i], hsend.at[i], hrecv.at[i], device_id=(nb,), device_id_type=MESH))
        asks[-1].start()

    for r0 in range(0, fan_one, 8):
        nr = min(8, fan_one - r0)
        for c0 in range(0, targets, 128):
            pos = n1_ref[r0:r0 + nr, c0:c0 + 128]
            if nr < 8:
                pos = jnp.broadcast_to(pos[0:1], (8, 128)) if nr == 1 else jnp.concatenate([pos, pos[0:8 - nr]], axis=0)
            hi = lax.shift_right_logical(pos, 7)
            lo = lax.bitwise_and(pos, 127)
            val = jnp.zeros((8, 128), I32)
            for h in range(ext.shape[0]):
                row = jnp.broadcast_to(ext[h:h + 1, :], (8, 128))
                val = jnp.where(hi == h, jnp.take_along_axis(row, lo, axis=1, mode='promise_in_bounds'), val)
            fld = jnp.zeros((8, 128), I32)
            for f in range(1, FIELDS):
                fld = fld + jnp.where(val >= f * width, 1, 0)
            idx[0, r0:r0 + 8, c0:c0 + 128] = val - fld * width
            idx[1, r0:r0 + 8, c0:c0 + 128] = lax.shift_left(jnp.ones((8, 128), I32), fld * FIELD_BITS)
    first = lanes_of(ext[0:targets // 128, :])
    nf[:, 0:targets] = jnp.where(iota((nf.shape[0], targets), 0) == first, 1.0, 0.0).astype(BF16)

    for cp in asks:
        cp.wait_recv()
    lane = iota((1, 128), 1)
    want = jnp.where(lane < HALO, ask_in[0, 0:1, :], ask_in[1, 0:1, :])
    pick = jnp.where(iota((store, 128), 0) == want, 1.0, 0.0).astype(BF16)
    loads[0].wait()
    out = dot(x_ref[...], pick)
    top = out[0:hrows]
    bot = jnp.concatenate([out[hrows:feat], jnp.zeros((2 * hrows - feat, 128), F32)], axis=0)
    low = iota((hrows, 128), 1) < HALO
    rep[0] = jnp.where(low, top, pltpu.roll(bot, HALO, 1)).astype(BF16)
    rep[1] = jnp.where(low, pltpu.roll(top, HALO, 1), bot).astype(BF16)
    reps = []
    for i, nb in enumerate((right, left)):
        reps.append(pltpu.make_async_remote_copy(rep.at[i], rep_in.at[i], hsend.at[2 + i], hrecv.at[2 + i], device_id=(nb,), device_id_type=MESH))
        reps[-1].start()

    block = 16

    def count_block(b, carry):
        base = pl.multiple_of(b * block, block)
        for c0 in range(0, targets, 256):
            row = iota((block, 256), 0) + base
            tot = jnp.zeros((block, 256), I32)
            for k in range(fan_one):
                tot = tot + jnp.where(row == idx[0, k:k + 1, c0:c0 + 256], idx[1, k:k + 1, c0:c0 + 256], 0)
            acc[pl.ds(base, block), c0:c0 + 256] = tot
        return carry

    lax.fori_loop(0, width // block, count_block, 0)
    for f in range(FIELDS):
        cnt = lax.bitwise_and(lax.shift_right_logical(acc[...], f * FIELD_BITS), (1 << FIELD_BITS) - 1)
        nf[f * width:(f + 1) * width, targets:2 * targets] = cnt.astype(F32).astype(BF16)
    both[...] = dot(x_ref[...], nf[0:store, :])

    small[...] = jnp.full(small.shape, -1, I32)
    small[0:fan_two, 0:seeds] = n2_ref[...]
    small[12:13, 0:seeds] = lab_ref[...]
    m2 = jnp.zeros((targets, 128), F32)
    for k in range(fan_two):
        m2 = m2 + jnp.where(iota((targets, 128), 0) == small[k:k + 1, :], 1.0, 0.0)
    m2 = m2.astype(BF16)

    for cp in reps:
        cp.wait_recv()
    from_l, from_r = rep_in[0].astype(F32), rep_in[1].astype(F32)
    halo = jnp.concatenate([jnp.where(low, from_l, pltpu.roll(from_r, HALO, 1)).astype(BF16),
                            jnp.where(low, pltpu.roll(from_l, HALO, 1), from_r).astype(BF16)], axis=0)
    rows = both[...] + dot(halo[0:feat], nf[store:store + 2 * HALO, :])
    x_t = rows[:, 0:targets].astype(BF16)
    a_t = (rows[:, targets:] * (1.0 / fan_one)).astype(BF16)
    loads[1].wait()
    loads[2].wait()
    z = dot(ws1_ref[...], x_t, 0, 0) + dot(wn1_ref[...], a_t, 0, 0)
    z_ref[...] = z
    h = jnp.maximum(z, 0.0).astype(BF16)
    a2 = (dot(h, m2) * (1.0 / fan_two)).astype(BF16)
    hs = h[:, 0:128]
    ws2, wn2 = ws2_ref[...], wn2_ref[...]
    logits = dot(ws2, hs) + dot(wn2, a2)
    shifted = logits - jnp.max(logits, axis=0, keepdims=True)
    log_prob = shifted - jnp.log(jnp.sum(jnp.exp(shifted), axis=0, keepdims=True))
    hit = iota(logits.shape, 0) == small[12:13, :]
    loss = -jnp.sum(jnp.where(hit, log_prob, 0.0))
    gl = (jnp.exp(log_prob) - jnp.where(hit, 1.0, 0.0)) * scale
    gpad[...] = jnp.zeros(gpad.shape, F32)
    gpad[0:classes, :] = jnp.where(lane < seeds, gl, 0.0)
    gb = gpad[...].astype(BF16)
    d_s2 = dot(gb, hs, 1, 1)
    d_n2 = dot(gb, a2, 1, 1)
    d_s2 = jnp.where(iota(d_s2.shape, 0) == classes, loss, d_s2)
    gc = gb[0:classes]
    g_seed = dot(ws2, gc, 0, 0)
    g_agg = dot(wn2, gc, 0, 0) * (1.0 / fan_two)
    p0 = g_agg.astype(BF16)
    r1 = g_agg - p0.astype(F32)
    p1 = r1.astype(BF16)
    p2 = (r1 - p1.astype(F32)).astype(BF16)
    d_h = dot(p0, m2, 1, 1) + (dot(p1, m2, 1, 1) + dot(p2, m2, 1, 1))
    d_h = d_h + jnp.concatenate([g_seed, jnp.zeros((g_seed.shape[0], targets - 128), F32)], axis=1)
    d_z = jnp.where(z_ref[...] > 0, d_h, 0.0).astype(BF16)
    tail = jnp.zeros((2 * hrows - feat, d_z.shape[0]), F32)
    at = 0
    for mat in (jnp.concatenate([dot(x_t, d_z, 1, 1), tail], axis=0),
                jnp.concatenate([dot(a_t, d_z, 1, 1), tail], axis=0), d_s2, d_n2):
        n = mat.shape[0] // 8
        for c0 in range(0, mat.shape[1], 128):
            g[at:at + n] = mat[:, c0:c0 + 128].reshape(n, 8, 128)
            at += n
    g[at:] = jnp.zeros((g.shape[0] - at, 8, 128), F32)

    copies = []

    def put(src, dst, to):
        k = len(copies)
        cp = pltpu.make_async_remote_copy(src, dst, send.at[k], recv.at[k], device_id=(to,), device_id_type=MESH)
        cp.start()
        copies.append(cp)
        return cp

    pieces = []
    for i in range(max(nx, ny)):
        if i < nx:
            d = (i + 1) % nx
            pieces.append((0, d, xs[d] * cx, cx))
        if i < ny:
            d = (i + 1) % ny
            pieces.append((1, d, off_b + ys[d] * cy, cy))
    other, mine = (1 - core) * half, core * half
    arrive = [put(g.at[pl.ds(other + o, n)], rc.at[pl.ds(o, n)], mate) for _, _, o, n in pieces]
    in_a, in_b = [], []
    for (kind, d, o, n), cp in zip(pieces, arrive):
        cp.wait_recv()
        part[pl.ds(o, n)] = g[pl.ds(mine + o, n)] + rc[pl.ds(o, n)]
        if d:
            if kind == 0:
                in_a.append((put(part.at[pl.ds(o, n)], l1a.at[d - 1], xdev[d]), d - 1))
            else:
                in_b.append((put(part.at[pl.ds(o, n)], l1b.at[d - 1], ydev[d]), d - 1))
    tot = part[pl.ds(mx * cx, cx)]
    for cp, s in in_a:
        cp.wait_recv()
        tot = tot + l1a[s]
    w2a[...] = tot
    in_a = [(put(w2a.at[pl.ds(ys[d] * ca, ca)], l2a.at[d - 1], ydev[d]), d - 1) for d in range(1, ny)]
    tot = part[pl.ds(off_b + my * cy, cy)]
    for cp, s in in_b:
        cp.wait_recv()
        tot = tot + l1b[s]
    w2b[...] = tot
    in_b = [(put(w2b.at[pl.ds(xs[d] * cb, cb)], l2b.at[d - 1], xdev[d]), d - 1) for d in range(1, nx)]
    tot = w2a[pl.ds(my * ca, ca)]
    for cp, s in in_a:
        cp.wait_recv()
        tot = tot + l2a[s]
    zc[0:ca] = tot
    tot = w2b[pl.ds(mx * cb, cb)]
    for cp, s in in_b:
        cp.wait_recv()
        tot = tot + l2b[s]
    zc[ca:zn] = tot
    in_z = [put(zc.at[pl.ds((zn * zs[d]) // nz, zsize)], lz.at[d - 1], zdev[d]) for d in range(1, nz)]
    tot = zc[pl.ds((zn * mz) // nz, zsize)]
    for s, cp in enumerate(in_z):
        cp.wait_recv()
        tot = tot + lz[s]
    zg[mz] = tot
    in_z = [put(zg.at[mz], zg.at[mz], zdev[d]) for d in range(1, nz)]
    for cp in in_z:
        cp.wait_recv()
    at_a = mine + mx * cx + my * ca
    at_b = mine + off_b + my * cy + mx * cb
    for z in range(nz):
        lo = (zn * z) // nz
        end = (zn * (z + 1)) // nz if z + 1 < nz else zn
        for t in range(lo, end):
            at = at_a + t if t < ca else at_b + (t - ca)
            full[pl.ds(at, 1)] = zg[z, t - lo:t - lo + 1]
    in_a = [put(full.at[pl.ds(at_a, ca)], full.at[pl.ds(at_a, ca)], ydev[d]) for d in range(1, ny)]
    in_b = [put(full.at[pl.ds(at_b, cb)], full.at[pl.ds(at_b, cb)], xdev[d]) for d in range(1, nx)]
    row_a, row_b = mine + mx * cx, mine + off_b + my * cy
    for cp in in_a:
        cp.wait_recv()
    in_a = [put(full.at[pl.ds(row_a, cx)], full.at[pl.ds(row_a, cx)], xdev[d]) for d in range(1, nx)]
    for cp in in_b:
        cp.wait_recv()
    in_b = [put(full.at[pl.ds(row_b, cy)], full.at[pl.ds(row_b, cy)], ydev[d]) for d in range(1, ny)]
    back = [put(full.at[pl.ds(row_a, cx)], full.at[pl.ds(row_a, cx)], mate),
            put(full.at[pl.ds(row_b, cy)], full.at[pl.ds(row_b, cy)], mate)]
    for i in range(max(nx, ny) - 1):
        if i < nx - 1:
            in_a[i].wait_recv()
            at = mine + lax.rem(mx + nx - 1 - i, nx) * cx
            back.append(put(full.at[pl.ds(at, cx)], full.at[pl.ds(at, cx)], mate))
        if i < ny - 1:
            in_b[i].wait_recv()
            at = mine + off_b + lax.rem(my + ny - 1 - i, ny) * cy
            back.append(put(full.at[pl.ds(at, cy)], full.at[pl.ds(at, cy)], mate))
    for cp in back:
        cp.wait_recv()
    for cp in copies:
        cp.wait_send()
    for cp in asks + reps:
        cp.wait_send()
    r_ref[...] = full[...]


def copy_count(group):
    nx, ny, nz = dims_of(group)
    return 2 * (nx + ny) + 4 * (nx - 1 + ny - 1) + 2 * (nz - 1)


def output_kernel(scale, r_ref, loss_ref, s1_ref, n1_ref, s2_ref, n2_ref):
    at = 0
    classes = s2_ref.shape[0]
    for ref in (s1_ref, n1_ref, s2_ref, n2_ref):
        rows, cols = ref.shape
        n = -(-rows // 8)
        for c0 in range(0, cols, 128):
            val = r_ref[at:at + n].reshape(n * 8, 128)
            ref[:, c0:c0 + 128] = val[0:rows]
            if ref is s2_ref and c0 == 0:
                loss_ref[...] = val[classes:classes + 1, 0:1] * scale
            at += n


def solution(mesh):
    group = mesh.shape['g']

    def device_step(x_local, front_ids, nbr_one, nbr_two, labels, w_self1, w_nbr1, w_self2, w_nbr2):
        store, feat = x_local.shape
        targets, fan_one = nbr_one.shape
        seeds = nbr_two.shape[0]
        hidden, classes = w_self2.shape
        frows = -(-feat // 32) * 32
        scale = 1.0 / (group * seeds)
        fid = front_ids.reshape(-1, 128)
        width = -(-(store + 2 * HALO) // (FIELDS * 16)) * 16
        nx, ny, nz = dims_of(group)
        ca, cb = chunks_of(group)
        cx, cy, zn = ny * ca, nx * cb, ca + cb
        zsize = -(-zn // nz)
        half = nx * cx + ny * cy
        total = 2 * half
        n = copy_count(group)
        dma = pltpu.SemaphoreType.DMA

        def buf(*lead):
            return VMEM((*lead, 8, 128), F32)

        vm, hbm = pl.BlockSpec(memory_space=VMEM), pl.BlockSpec(memory_space=pl.ANY)
        sums = pl.pallas_call(
            functools.partial(step_kernel, group, scale),
            name='train_step',
            out_shape=jax.ShapeDtypeStruct((total, 8, 128), F32),
            in_specs=[vm, hbm, vm, vm, vm, hbm, hbm, vm, vm],
            out_specs=vm,
            scratch_shapes=[
                VMEM((feat, store), BF16), VMEM((feat, hidden), BF16), VMEM((feat, hidden), BF16), dma((3,)),
                VMEM((8, 128), I32), VMEM((2, 8, 128), I32), VMEM((2, frows // 2, 128), BF16),
                VMEM((2, frows // 2, 128), BF16), dma((4,)), dma((4,)),
                VMEM((16, 128), I32), VMEM((2, -(-fan_one // 8) * 8, targets), I32), VMEM((width, targets), I32),
                VMEM((FIELDS * width, 2 * targets), BF16), VMEM((feat, 2 * targets), F32), VMEM((hidden, targets), F32),
                VMEM((-(-classes // 16) * 16, 128), F32), buf(total),
                buf(half), buf(half), buf(nx - 1, cx), buf(ny - 1, cy), buf(cx), buf(cy),
                buf(ny - 1, ca), buf(nx - 1, cb), buf(zn), buf(nz - 1, zsize), buf(nz, zsize), buf(total),
                dma((n,)), dma((n,))],
            compiler_params=pltpu.CompilerParams(collective_id=0, has_side_effects=True,
                                                 vmem_limit_bytes=60 * 1024 * 1024),
        )(fid, x_local.T, nbr_one.T, nbr_two.T, labels.reshape(1, -1), w_self1, w_nbr1, w_self2.T, w_nbr2.T)
        loss, d_s1, d_n1, d_s2, d_n2 = pl.pallas_call(
            functools.partial(output_kernel, scale),
            name='split_outputs',
            out_shape=[jax.ShapeDtypeStruct((1, 1), F32), jax.ShapeDtypeStruct((feat, hidden), F32),
                       jax.ShapeDtypeStruct((feat, hidden), F32), jax.ShapeDtypeStruct((classes, hidden), F32),
                       jax.ShapeDtypeStruct((classes, hidden), F32)],
            in_specs=[vm], out_specs=[vm] * 5,
        )(sums)
        return loss[0, 0], d_s1, d_n1, d_s2.T, d_n2.T

    return jax.shard_map(device_step, mesh=mesh,
                         in_specs=(P('g', None), P('g'), P('g', None), P('g', None), P('g'), P(), P(), P(), P()),
                         out_specs=(P(), P(), P(), P(), P()), check_vma=False)
```

time: 76.3 us -> 64.9 us (0.85)
  Pallas kernels: 75.5 us -> 64.1 us
    pallas_call x3 -> x1, Pallas kernels: 73 us -> 61.6 us  [device_step(): pl.pallas_call(functools.partial(step_kernel, group, scale), name='train_...]
where the time goes in v2:
time: 64.9 us; the launch traced here: 64.7 us
  Pallas kernels  64.1 us (99%)
    pallas_call x1, Pallas kernels, device_step(): pl.pallas_call(functools.partial(step_kernel, group, scale), name='train_...  61.6 us
    pallas_call x1, Pallas kernels, device_step(): pl.pallas_call(functools.partial(output_kernel, scale), name='split_outpu...  2.46 us

profile of v2, /device:TPU:1, one launch (start us, length us, event | category | flops | bytes accessed | tf_op | source)
XLA Modules:
  0.0 64.7 jit_solution(14087207593718118924)
XLA Ops:
  0.6 61.6 %train_step.1.r_ref = f32[352,8,128]{2,1,0:T(8,128)} custom-call(s32[16,128]{1,0:T(8,128)} %bitcast.14, bf16[602,2048]{1,0:T(8,128)(2,1)} %bitcast.10, s32[25,512]{1,0:T(8,128)} %bitcast.11, s32[10,64]{1,0:T(8,128)} %bitcast.15, s32[1,64]{1,0:T(1,128)} %bitcast.16, bf16[602,256]{1,0:T(8,128)(2,1)} %ws1_hbm.1, bf16[602,256]{1,0:T(8,128)(2,1)} %wn1_hbm.1, ...), custom_call_target="tpu_custom_call" | custom-call | tf_op jit(solution)/shard_map/train_step/pallas_call | solution.py:371
  62.3 2.5 %split_outputs.1 = (f32[1,1]{1,0:T(1,128)}, f32[602,256]{1,0:T(8,128)}, f32[602,256]{1,0:T(8,128)}, f32[41,256]{1,0:T(8,128)}, f32[41,256]{1,0:T(8,128)}) custom-call(f32[352,8,128]{2,1,0:T(8,128)} %train_step.1.r_ref), custom_call_target="tpu_custom_call" | custom-call | tf_op jit(solution)/shard_map/split_outputs/pallas_call | solution.py:390

commit v3 on v2

--- a/solution.py
+++ b/solution.py
@@ -72,7 +72,8 @@
     nx, ny, nz = dims_of(group)
     ca, cb = chunks_of(group)
     cx, cy, zn = ny * ca, nx * cb, ca + cb
-    zsize = -(-zn // nz)
+    nq = max(1, nz // 2)
+    zsize = -(-zn // nq)
     off_b = nx * cx
     half = off_b + ny * cy
     me = lax.axis_index('g')
@@ -226,7 +227,8 @@
         for c0 in range(0, mat.shape[1], 128):
             g[at:at + n] = mat[:, c0:c0 + 128].reshape(n, 8, 128)
             at += n
-    g[at:] = jnp.zeros((g.shape[0] - at, 8, 128), F32)
+    if at < g.shape[0]:
+        g[at:] = jnp.zeros((g.shape[0] - at, 8, 128), F32)
 
     copies = []
 
@@ -237,96 +239,104 @@
         copies.append(cp)
         return cp
 
+    other, mine = (1 - core) * half, core * half
+    part_a = (nx, xs, xdev, cx, 0, ny, ys, ydev, ca, l1a, w2a, l2a)
+    part_b = (ny, ys, ydev, cy, off_b, nx, xs, xdev, cb, l1b, w2b, l2b)
+    parts = (part_a, part_b)
     pieces = []
     for i in range(max(nx, ny)):
-        if i < nx:
-            d = (i + 1) % nx
-            pieces.append((0, d, xs[d] * cx, cx))
-        if i < ny:
-            d = (i + 1) % ny
-            pieces.append((1, d, off_b + ys[d] * cy, cy))
-    other, mine = (1 - core) * half, core * half
-    arrive = [put(g.at[pl.ds(other + o, n)], rc.at[pl.ds(o, n)], mate) for _, _, o, n in pieces]
-    in_a, in_b = [], []
-    for (kind, d, o, n), cp in zip(pieces, arrive):
+        for w, p in enumerate(parts):
+            if i < p[0]:
+                d = (i + 1) % p[0]
+                pieces.append((w, d, p[4] + p[1][d] * p[3]))
+    arrive = [put(g.at[pl.ds(other + o, parts[w][3])], rc.at[pl.ds(o, parts[w][3])], mate) for w, d, o in pieces]
+    first_in = [{}, {}]
+    for (w, d, o), cp in zip(pieces, arrive):
+        _, _, to, n, _, n2, sub, _, c, land, _, _ = parts[w]
         cp.wait_recv()
         part[pl.ds(o, n)] = g[pl.ds(mine + o, n)] + rc[pl.ds(o, n)]
         if d:
-            if kind == 0:
-                in_a.append((put(part.at[pl.ds(o, n)], l1a.at[d - 1], xdev[d]), d - 1))
-            else:
-                in_b.append((put(part.at[pl.ds(o, n)], l1b.at[d - 1], ydev[d]), d - 1))
-    tot = part[pl.ds(mx * cx, cx)]
-    for cp, s in in_a:
-        cp.wait_recv()
-        tot = tot + l1a[s]
-    w2a[...] = tot
-    in_a = [(put(w2a.at[pl.ds(ys[d] * ca, ca)], l2a.at[d - 1], ydev[d]), d - 1) for d in range(1, ny)]
-    tot = part[pl.ds(off_b + my * cy, cy)]
-    for cp, s in in_b:
-        cp.wait_recv()
-        tot = tot + l1b[s]
-    w2b[...] = tot
-    in_b = [(put(w2b.at[pl.ds(xs[d] * cb, cb)], l2b.at[d - 1], xdev[d]), d - 1) for d in range(1, nx)]
-    tot = w2a[pl.ds(my * ca, ca)]
-    for cp, s in in_a:
-        cp.wait_recv()
-        tot = tot + l2a[s]
-    zc[0:ca] = tot
-    tot = w2b[pl.ds(mx * cb, cb)]
-    for cp, s in in_b:
-        cp.wait_recv()
-        tot = tot + l2b[s]
-    zc[ca:zn] = tot
-    in_z = [put(zc.at[pl.ds((zn * zs[d]) // nz, zsize)], lz.at[d - 1], zdev[d]) for d in range(1, nz)]
-    tot = zc[pl.ds((zn * mz) // nz, zsize)]
-    for s, cp in enumerate(in_z):
-        cp.wait_recv()
-        tot = tot + lz[s]
-    zg[mz] = tot
-    in_z = [put(zg.at[mz], zg.at[mz], zdev[d]) for d in range(1, nz)]
+            for i in range(n2):
+                e = (i + 1) % n2
+                first_in[w][d, e] = put(part.at[pl.ds(o + sub[e] * c, c)], land.at[d - 1, e], to[d])
+    second_in, sums = [[], []], [None, None]
+    for i in range(max(nx, ny)):
+        for w, (n1, own, _, n, off, n2, sub, to, c, land, w2, l2) in enumerate(parts):
+            if i < n2:
+                e = (i + 1) % n2
+                tot = part[pl.ds(off + own[0] * n + sub[e] * c, c)]
+                for d in range(1, n1):
+                    first_in[w][d, e].wait_recv()
+                    tot = tot + land[d - 1, e]
+                if e:
+                    w2[e - 1] = tot
+                    second_in[w].append(put(w2.at[e - 1], l2.at[e - 1], to[e]))
+                else:
+                    sums[w] = tot
+    for w, at, n in ((0, 0, ca), (1, ca, cb)):
+        tot = sums[w]
+        for e, cp in enumerate(second_in[w]):
+            cp.wait_recv()
+            tot = tot + parts[w][11][e]
+        zc[at:at + n] = tot
+    quarter = lax.rem(mz, nq)
+    in_z = [put(zc.at[pl.ds((zn * lax.rem(zs[d], nq)) // nq, zsize)], lz.at[mz], zdev[d]) for d in range(1, nz)]
+    lz[mz] = zc[pl.ds((zn * quarter) // nq, zsize)]
     for cp in in_z:
         cp.wait_recv()
-    at_a = mine + mx * cx + my * ca
-    at_b = mine + off_b + my * cy + mx * cb
-    for z in range(nz):
-        lo = (zn * z) // nz
-        end = (zn * (z + 1)) // nz if z + 1 < nz else zn
+    tot = lz[0]
+    for z in range(1, nz):
+        tot = tot + lz[z]
+    zg[quarter] = tot
+    if nq == 4:
+        far = lax.rem(mz + 2 + 4 * lax.rem(mz, 2), nz)
+        targets_z = (zdev[1], zdev[nz - 1], dev(far, my, mx, core))
+        in_z = [put(zg.at[quarter], zg.at[quarter], to) for to in targets_z]
+        for cp in in_z:
+            cp.wait_recv()
+    base = [mine + p[4] + p[1][0] * p[3] for p in parts]
+    spots = [base[w] + p[6][0] * p[8] for w, p in enumerate(parts)]
+    for q in range(nq):
+        lo = (zn * q) // nq
+        end = (zn * (q + 1)) // nq
         for t in range(lo, end):
-            at = at_a + t if t < ca else at_b + (t - ca)
-            full[pl.ds(at, 1)] = zg[z, t - lo:t - lo + 1]
-    in_a = [put(full.at[pl.ds(at_a, ca)], full.at[pl.ds(at_a, ca)], ydev[d]) for d in range(1, ny)]
-    in_b = [put(full.at[pl.ds(at_b, cb)], full.at[pl.ds(at_b, cb)], xdev[d]) for d in range(1, nx)]
-    row_a, row_b = mine + mx * cx, mine + off_b + my * cy
-    for cp in in_a:
-        cp.wait_recv()
-    in_a = [put(full.at[pl.ds(row_a, cx)], full.at[pl.ds(row_a, cx)], xdev[d]) for d in range(1, nx)]
-    for cp in in_b:
-        cp.wait_recv()
-    in_b = [put(full.at[pl.ds(row_b, cy)], full.at[pl.ds(row_b, cy)], ydev[d]) for d in range(1, ny)]
-    back = [put(full.at[pl.ds(row_a, cx)], full.at[pl.ds(row_a, cx)], mate),
-            put(full.at[pl.ds(row_b, cy)], full.at[pl.ds(row_b, cy)], mate)]
-    for i in range(max(nx, ny) - 1):
-        if i < nx - 1:
-            in_a[i].wait_recv()
-            at = mine + lax.rem(mx + nx - 1 - i, nx) * cx
-            back.append(put(full.at[pl.ds(at, cx)], full.at[pl.ds(at, cx)], mate))
-        if i < ny - 1:
-            in_b[i].wait_recv()
-            at = mine + off_b + lax.rem(my + ny - 1 - i, ny) * cy
-            back.append(put(full.at[pl.ds(at, cy)], full.at[pl.ds(at, cy)], mate))
+            at = spots[0] + t if t < ca else spots[1] + (t - ca)
+            full[pl.ds(at, 1)] = zg[q, t - lo:t - lo + 1]
+    back = []
+
+    def spread(w, at):
+        n1, _, to, _, _, _, _, _, c, _, _, _ = parts[w]
+        got = [put(full.at[pl.ds(at, c)], full.at[pl.ds(at, c)], to[d]) for d in range(1, n1)]
+        back.append(put(full.at[pl.ds(at, c)], full.at[pl.ds(at, c)], mate))
+        return got
+
+    second_in = [[], []]
+    for w, p in enumerate(parts):
+        for e in range(1, p[5]):
+            second_in[w].append(put(full.at[pl.ds(spots[w], p[8])], full.at[pl.ds(spots[w], p[8])], p[7][e]))
+    first_in = [[spread(w, spots[w])] for w in range(2)]
+    for i in range(max(nx, ny)):
+        for w, (n1, own, _, n, off, n2, sub, _, c, _, _, _) in enumerate(parts):
+            if i < n2 - 1:
+                second_in[w][i].wait_recv()
+                first_in[w].append(spread(w, base[w] + sub[n2 - 1 - i] * c))
+    for i in range(max(nx, ny)):
+        for w, (n1, own, _, n, off, n2, sub, _, c, _, _, _) in enumerate(parts):
+            if i < n2:
+                for d in range(1, n1):
+                    first_in[w][i][d - 1].wait_recv()
+                    at = mine + off + own[n1 - d] * n + sub[(n2 - i) % n2] * c
+                    back.append(put(full.at[pl.ds(at, c)], full.at[pl.ds(at, c)], mate))
     for cp in back:
         cp.wait_recv()
-    for cp in copies:
-        cp.wait_send()
-    for cp in asks + reps:
+    for cp in copies + asks + reps:
         cp.wait_send()
     r_ref[...] = full[...]
 
 
 def copy_count(group):
     nx, ny, nz = dims_of(group)
-    return 2 * (nx + ny) + 4 * (nx - 1 + ny - 1) + 2 * (nz - 1)
+    return nx + ny + 2 * ((nx - 1) * ny + (ny - 1) * nx + nx - 1 + ny - 1) + nz - 1 + (3 if nz == 8 else 0) + 2 * nx * ny
 
 
 def output_kernel(scale, r_ref, loss_ref, s1_ref, n1_ref, s2_ref, n2_ref):
@@ -358,7 +368,8 @@
         nx, ny, nz = dims_of(group)
         ca, cb = chunks_of(group)
         cx, cy, zn = ny * ca, nx * cb, ca + cb
-        zsize = -(-zn // nz)
+        nq = max(1, nz // 2)
+        zsize = -(-zn // nq)
         half = nx * cx + ny * cy
         total = 2 * half
         n = copy_count(group)
@@ -381,8 +392,8 @@
                 VMEM((16, 128), I32), VMEM((2, -(-fan_one // 8) * 8, targets), I32), VMEM((width, targets), I32),
                 VMEM((FIELDS * width, 2 * targets), BF16), VMEM((feat, 2 * targets), F32), VMEM((hidden, targets), F32),
                 VMEM((-(-classes // 16) * 16, 128), F32), buf(total),
-                buf(half), buf(half), buf(nx - 1, cx), buf(ny - 1, cy), buf(cx), buf(cy),
-                buf(ny - 1, ca), buf(nx - 1, cb), buf(zn), buf(nz - 1, zsize), buf(nz, zsize), buf(total),
+                buf(half), buf(half), buf(nx - 1, ny, ca), buf(ny - 1, nx, cb), buf(ny - 1, ca), buf(nx - 1, cb),
+                buf(ny - 1, ca), buf(nx - 1, cb), buf(zn), buf(nz, zsize), buf(nq, zsize), buf(total),
                 dma((n,)), dma((n,))],
             compiler_params=pltpu.CompilerParams(collective_id=0, has_side_effects=True,
                                                  vmem_limit_bytes=60 * 1024 * 1024),

time: 64.9 us -> 61.8 us (0.952)
  Pallas kernels: 64.1 us -> 61 us
    pallas_call x1, Pallas kernels: 61.6 us -> 58.5 us  [device_step(): pl.pallas_call(functools.partial(step_kernel, group, scale), name='train_...]
where the time goes in v3:
time: 61.8 us; the launch traced here: 61.6 us
  Pallas kernels  61 us (99%)
  between operations  0.64 us (1%)
    pallas_call x1, Pallas kernels, device_step(): pl.pallas_call(functools.partial(step_kernel, group, scale), name='train_...  58.5 us
    pallas_call x1, Pallas kernels, device_step(): pl.pallas_call(functools.partial(output_kernel, scale), name='split_outpu...  2.46 us

profile of v3, /device:TPU:1, one launch (start us, length us, event | category | flops | bytes accessed | tf_op | source)
XLA Modules:
  0.0 61.6 jit_solution(3900159641016463338)
XLA Ops:
  0.6 58.5 %train_step.1.r_ref = f32[352,8,128]{2,1,0:T(8,128)} custom-call(s32[16,128]{1,0:T(8,128)} %bitcast.14, bf16[602,2048]{1,0:T(8,128)(2,1)} %bitcast.10, s32[25,512]{1,0:T(8,128)} %bitcast.11, s32[10,64]{1,0:T(8,128)} %bitcast.15, s32[1,64]{1,0:T(1,128)} %bitcast.16, bf16[602,256]{1,0:T(8,128)(2,1)} %ws1_hbm.1, bf16[602,256]{1,0:T(8,128)(2,1)} %wn1_hbm.1, ...), custom_call_target="tpu_custom_call" | custom-call | tf_op jit(solution)/shard_map/train_step/pallas_call | solution.py:382
  59.1 2.5 %split_outputs.1 = (f32[1,1]{1,0:T(1,128)}, f32[602,256]{1,0:T(8,128)}, f32[602,256]{1,0:T(8,128)}, f32[41,256]{1,0:T(8,128)}, f32[41,256]{1,0:T(8,128)}) custom-call(f32[352,8,128]{2,1,0:T(8,128)} %train_step.1.r_ref), custom_call_target="tpu_custom_call" | custom-call | tf_op jit(solution)/shard_map/split_outputs/pallas_call | solution.py:401

commit v4 on v3

--- a/solution.py
+++ b/solution.py
@@ -65,8 +65,9 @@
     return got[0:1] * 64 + got[1:2]
 
 
-def step_kernel(group, scale, fid_ref, x_hbm, n1_ref, n2_ref, lab_ref, ws1_hbm, wn1_hbm, ws2_ref, wn2_ref, r_ref,
-                x_ref, ws1_ref, wn1_ref, in_sem, ask, ask_in, rep, rep_in, hsend, hrecv,
+def step_kernel(group, scale, fid_hbm, x_hbm, n1_hbm, n2_hbm, lab_hbm, ws1_hbm, wn1_hbm, ws2_hbm, wn2_hbm, r_ref,
+                fid_ref, x_ref, n1_ref, n2_ref, lab_ref, ws1_ref, wn1_ref, ws2_ref, wn2_ref, in_sem,
+                ws1_t, wn1_t, ws2_t, wn2_t, ask, ask_in, rep, rep_in, hsend, hrecv,
                 small, idx, acc, nf, both, z_ref, gpad, g,
                 rc, part, l1a, l1b, w2a, w2b, l2a, l2b, zc, lz, zg, full, send, recv):
     nx, ny, nz = dims_of(group)
@@ -98,8 +99,9 @@
     peers = [left, right, mate] + xdev[1:] + ydev[1:] + zdev[1:]
     for nb in peers:
         pl.semaphore_signal(barrier, inc=1, device_id=(nb,), device_id_type=MESH)
-    loads = [pltpu.make_async_copy(s, d, in_sem.at[i]) for i, (s, d) in
-             enumerate(((x_hbm, x_ref), (ws1_hbm, ws1_ref), (wn1_hbm, wn1_ref)))]
+    loads = [pltpu.make_async_copy(src, dst, in_sem.at[i]) for i, (src, dst) in
+             enumerate(((fid_hbm, fid_ref), (n1_hbm, n1_ref), (x_hbm, x_ref), (n2_hbm, n2_ref), (lab_hbm, lab_ref),
+                        (ws1_hbm, ws1_ref), (wn1_hbm, wn1_ref), (ws2_hbm, ws2_ref), (wn2_hbm, wn2_ref)))]
     for cp in loads:
         cp.start()
 
@@ -110,6 +112,7 @@
     classes = ws2_ref.shape[0]
     width = acc.shape[0]
     hrows = rep.shape[1]
+    loads[0].wait()
     ext, off = frontier_ext(fid_ref[...], me, group, store.bit_length() - 1)
     ask[...] = jnp.broadcast_to(ask_rows(ext, off, store), ask.shape)
     pl.semaphore_wait(barrier, len(peers))
@@ -118,6 +121,7 @@
         asks.append(pltpu.make_async_remote_copy(ask, ask_in.at[i], hsend.at[i], hrecv.at[i], device_id=(nb,), device_id_type=MESH))
         asks[-1].start()
 
+    loads[1].wait()
     for r0 in range(0, fan_one, 8):
         nr = min(8, fan_one - r0)
         for c0 in range(0, targets, 128):
@@ -143,7 +147,7 @@
     lane = iota((1, 128), 1)
     want = jnp.where(lane < HALO, ask_in[0, 0:1, :], ask_in[1, 0:1, :])
     pick = jnp.where(iota((store, 128), 0) == want, 1.0, 0.0).astype(BF16)
-    loads[0].wait()
+    loads[2].wait()
     out = dot(x_ref[...], pick)
     top = out[0:hrows]
     bot = jnp.concatenate([out[hrows:feat], jnp.zeros((2 * hrows - feat, 128), F32)], axis=0)
@@ -173,6 +177,8 @@
         nf[f * width:(f + 1) * width, targets:2 * targets] = cnt.astype(F32).astype(BF16)
     both[...] = dot(x_ref[...], nf[0:store, :])
 
+    for cp in loads[3:]:
+        cp.wait()
     small[...] = jnp.full(small.shape, -1, I32)
     small[0:fan_two, 0:seeds] = n2_ref[...]
     small[12:13, 0:seeds] = lab_ref[...]
@@ -180,6 +186,8 @@
     for k in range(fan_two):
         m2 = m2 + jnp.where(iota((targets, 128), 0) == small[k:k + 1, :], 1.0, 0.0)
     m2 = m2.astype(BF16)
+    for src, dst in ((ws1_ref, ws1_t), (wn1_ref, wn1_t), (ws2_ref, ws2_t), (wn2_ref, wn2_t)):
+        dst[...] = src[...].T
 
     for cp in reps:
         cp.wait_recv()
@@ -189,9 +197,7 @@
     rows = both[...] + dot(halo[0:feat], nf[store:store + 2 * HALO, :])
     x_t = rows[:, 0:targets].astype(BF16)
     a_t = (rows[:, targets:] * (1.0 / fan_one)).astype(BF16)
-    loads[1].wait()
-    loads[2].wait()
-    z = dot(ws1_ref[...], x_t, 0, 0) + dot(wn1_ref[...], a_t, 0, 0)
+    z = dot(ws1_t[...], x_t) + dot(wn1_t[...], a_t)
     z_ref[...] = z
     h = jnp.maximum(z, 0.0).astype(BF16)
     a2 = (dot(h, m2) * (1.0 / fan_two)).astype(BF16)
@@ -210,8 +216,8 @@
     d_n2 = dot(gb, a2, 1, 1)
     d_s2 = jnp.where(iota(d_s2.shape, 0) == classes, loss, d_s2)
     gc = gb[0:classes]
-    g_seed = dot(ws2, gc, 0, 0)
-    g_agg = dot(wn2, gc, 0, 0) * (1.0 / fan_two)
+    g_seed = dot(ws2_t[...], gc)
+    g_agg = dot(wn2_t[...], gc) * (1.0 / fan_two)
     p0 = g_agg.astype(BF16)
     r1 = g_agg - p0.astype(F32)
     p1 = r1.astype(BF16)
@@ -339,18 +345,28 @@
     return nx + ny + 2 * ((nx - 1) * ny + (ny - 1) * nx + nx - 1 + ny - 1) + nz - 1 + (3 if nz == 8 else 0) + 2 * nx * ny
 
 
-def output_kernel(scale, r_ref, loss_ref, s1_ref, n1_ref, s2_ref, n2_ref):
-    at = 0
-    classes = s2_ref.shape[0]
-    for ref in (s1_ref, n1_ref, s2_ref, n2_ref):
+def output_kernel(scale, r_ref, loss_ref, s1_hbm, n1_hbm, s2_hbm, n2_hbm, s1, n1, s2, n2, sem):
+    at, k = 0, 0
+    classes = s2.shape[0]
+    copies = []
+    for ref, hbm in ((s1, s1_hbm), (n1, n1_hbm), (s2, s2_hbm), (n2, n2_hbm)):
         rows, cols = ref.shape
         n = -(-rows // 8)
-        for c0 in range(0, cols, 128):
-            val = r_ref[at:at + n].reshape(n * 8, 128)
-            ref[:, c0:c0 + 128] = val[0:rows]
-            if ref is s2_ref and c0 == 0:
-                loss_ref[...] = val[classes:classes + 1, 0:1] * scale
-            at += n
+        step = n if n < 16 else 19
+        for r0 in range(0, n, step):
+            lo, hi = r0 * 8, min(rows, (r0 + step) * 8)
+            for c in range(cols // 128):
+                val = r_ref[at + c * n + r0:at + c * n + r0 + step].reshape(step * 8, 128)
+                ref[lo:hi, c * 128:(c + 1) * 128] = val[0:hi - lo]
+                if ref is s2 and c == 0:
+                    loss_ref[...] = val[classes:classes + 1, 0:1] * scale
+            cp = pltpu.make_async_copy(ref.at[lo:hi], hbm.at[lo:hi], sem.at[k])
+            cp.start()
+            copies.append(cp)
+            k += 1
+        at += n * (cols // 128)
+    for cp in copies:
+        cp.wait()
 
 
 def solution(mesh):
@@ -359,7 +375,7 @@
     def device_step(x_local, front_ids, nbr_one, nbr_two, labels, w_self1, w_nbr1, w_self2, w_nbr2):
         store, feat = x_local.shape
         targets, fan_one = nbr_one.shape
-        seeds = nbr_two.shape[0]
+        seeds, fan_two = nbr_two.shape
         hidden, classes = w_self2.shape
         frows = -(-feat // 32) * 32
         scale = 1.0 / (group * seeds)
@@ -382,11 +398,14 @@
         sums = pl.pallas_call(
             functools.partial(step_kernel, group, scale),
             name='train_step',
-            out_shape=jax.ShapeDtypeStruct((total, 8, 128), F32),
-            in_specs=[vm, hbm, vm, vm, vm, hbm, hbm, vm, vm],
+            out_shape=VMEM((total, 8, 128), F32),
+            in_specs=[hbm] * 9,
             out_specs=vm,
             scratch_shapes=[
-                VMEM((feat, store), BF16), VMEM((feat, hidden), BF16), VMEM((feat, hidden), BF16), dma((3,)),
+                VMEM(fid.shape, I32), VMEM((feat, store), BF16), VMEM((fan_one, targets), I32), VMEM((fan_two, seeds), I32),
+                VMEM((1, seeds), I32), VMEM((feat, hidden), BF16), VMEM((feat, hidden), BF16), VMEM((classes, hidden), BF16),
+                VMEM((classes, hidden), BF16), dma((9,)),
+                VMEM((hidden, feat), BF16), VMEM((hidden, feat), BF16), VMEM((hidden, classes), BF16), VMEM((hidden, classes), BF16),
                 VMEM((8, 128), I32), VMEM((2, 8, 128), I32), VMEM((2, frows // 2, 128), BF16),
                 VMEM((2, frows // 2, 128), BF16), dma((4,)), dma((4,)),
                 VMEM((16, 128), I32), VMEM((2, -(-fan_one // 8) * 8, targets), I32), VMEM((width, targets), I32),
@@ -404,8 +423,10 @@
             out_shape=[jax.ShapeDtypeStruct((1, 1), F32), jax.ShapeDtypeStruct((feat, hidden), F32),
                        jax.ShapeDtypeStruct((feat, hidden), F32), jax.ShapeDtypeStruct((classes, hidden), F32),
                        jax.ShapeDtypeStruct((classes, hidden), F32)],
-            in_specs=[vm], out_specs=[vm] * 5,
-        )(sums)
+            in_specs=[vm], out_specs=[vm] + [hbm] * 4,
+            scratch_shapes=[VMEM((feat, hidden), F32), VMEM((feat, hidden), F32), VMEM((classes, hidden), F32),
+                            VMEM((classes, hidden), F32), dma((10,))],
+        )(pltpu.with_memory_space_constraint(sums, VMEM))
         return loss[0, 0], d_s1, d_n1, d_s2.T, d_n2.T
 
     return jax.shard_map(device_step, mesh=mesh,

time: 61.8 us -> 58.9 us (0.953)
  Pallas kernels: 61 us -> 58.1 us
    pallas_call x1, Pallas kernels: 58.5 us -> 56.5 us  [device_step(): pl.pallas_call(functools.partial(step_kernel, group, scale), name='train_...]
    pallas_call x1, Pallas kernels: 2.46 us -> 1.66 us  [device_step(): pl.pallas_call(functools.partial(output_kernel, scale), name='split_outpu...]
where the time goes in v4:
time: 58.9 us; the launch traced here: 58.8 us
  Pallas kernels  58.1 us (99%)
  between operations  0.64 us (1%)
    pallas_call x1, Pallas kernels, device_step(): pl.pallas_call(functools.partial(step_kernel, group, scale), name='train_...  56.5 us
    pallas_call x1, Pallas kernels, device_step(): pl.pallas_call(functools.partial(output_kernel, scale), name='split_outpu...  1.66 us

profile of v4, /device:TPU:1, one launch (start us, length us, event | category | flops | bytes accessed | tf_op | source)
XLA Modules:
  0.0 58.8 jit_solution(13573767945515708212)
XLA Ops:
  0.6 56.5 %train_step.1.r_ref = f32[352,8,128]{2,1,0:T(8,128)S(1)} custom-call(s32[16,128]{1,0:T(8,128)} %bitcast.14, bf16[602,2048]{1,0:T(8,128)(2,1)} %bitcast.10, s32[25,512]{1,0:T(8,128)} %bitcast.11, s32[10,64]{1,0:T(8,128)} %bitcast.15, s32[1,64]{1,0:T(1,128)} %bitcast.16, bf16[602,256]{1,0:T(8,128)(2,1)} %ws1_hbm.1, bf16[602,256]{1,0:T(8,128)(2,1)} %wn1_hbm.1, ...), custom_call_target="tpu_custom_call" | custom-call | tf_op jit(solution)/shard_map/train_step/pallas_call | solution.py:398
  57.1 1.7 %split_outputs.1 = (f32[1,1]{1,0:T(1,128)}, f32[602,256]{1,0:T(8,128)}, f32[602,256]{1,0:T(8,128)}, f32[41,256]{1,0:T(8,128)}, f32[41,256]{1,0:T(8,128)}) custom-call(f32[352,8,128]{2,1,0:T(8,128)S(1)} %train_step.1.r_ref), custom_call_target="tpu_custom_call" | custom-call | tf_op jit(solution)/shard_map/split_outputs/pallas_call | solution.py:420

commit v5 on v4

--- a/solution.py
+++ b/solution.py
@@ -67,9 +67,9 @@
 
 def step_kernel(group, scale, fid_hbm, x_hbm, n1_hbm, n2_hbm, lab_hbm, ws1_hbm, wn1_hbm, ws2_hbm, wn2_hbm, r_ref,
                 fid_ref, x_ref, n1_ref, n2_ref, lab_ref, ws1_ref, wn1_ref, ws2_ref, wn2_ref, in_sem,
-                ws1_t, wn1_t, ws2_t, wn2_t, ask, ask_in, rep, rep_in, hsend, hrecv,
+                ws1_t, wn1_t, ws2_t, wn2_t, ask, ask_in, rep, rep_in, hsend, hrecv, up,
                 small, idx, acc, nf, both, z_ref, gpad, g,
-                rc, part, l1a, l1b, w2a, w2b, l2a, l2b, zc, lz, zg, full, send, recv):
+                rc, part, l1a, l1b, w2a, w2b, l2a, l2b, zc, lz, zg, send, recv):
     nx, ny, nz = dims_of(group)
     ca, cb = chunks_of(group)
     cx, cy, zn = ny * ca, nx * cb, ca + cb
@@ -96,9 +96,15 @@
     left, right = lax.rem(me + group - 1, group), lax.rem(me + 1, group)
 
     barrier = pltpu.get_barrier_semaphore()
-    peers = [left, right, mate] + xdev[1:] + ydev[1:] + zdev[1:]
+    peers = [left, right, mate] + xdev[1:] + ydev[1:]
+
+    def signal(sem, to):
+        pl.semaphore_signal(sem, inc=1, device_id=(to,), device_id_type=MESH)
+
     for nb in peers:
         pl.semaphore_signal(barrier, inc=1, device_id=(nb,), device_id_type=MESH)
+    for d in range(1, nz):
+        pl.when(mz + d < nz)(functools.partial(signal, barrier, zdev[d]))
     loads = [pltpu.make_async_copy(src, dst, in_sem.at[i]) for i, (src, dst) in
              enumerate(((fid_hbm, fid_ref), (n1_hbm, n1_ref), (x_hbm, x_ref), (n2_hbm, n2_ref), (lab_hbm, lab_ref),
                         (ws1_hbm, ws1_ref), (wn1_hbm, wn1_ref), (ws2_hbm, ws2_ref), (wn2_hbm, wn2_ref)))]
@@ -115,11 +121,19 @@
     loads[0].wait()
     ext, off = frontier_ext(fid_ref[...], me, group, store.bit_length() - 1)
     ask[...] = jnp.broadcast_to(ask_rows(ext, off, store), ask.shape)
-    pl.semaphore_wait(barrier, len(peers))
     asks = []
     for i, nb in enumerate((left, right)):
         asks.append(pltpu.make_async_remote_copy(ask, ask_in.at[i], hsend.at[i], hrecv.at[i], device_id=(nb,), device_id_type=MESH))
-        asks[-1].start()
+
+    def ask_neighbours():
+        pl.semaphore_wait(barrier, len(peers) + mz)
+        for cp in asks:
+            cp.start()
+        for d in range(1, nz):
+            pl.when(mz + d >= nz)(functools.partial(signal, up.at[nz - d], zdev[d]))
+
+    first_of_plane = lax.rem(me, 2 * nx * ny) == 0
+    pl.when(jnp.logical_not(first_of_plane))(ask_neighbours)
 
     loads[1].wait()
     for r0 in range(0, fan_one, 8):
@@ -142,6 +156,37 @@
     first = lanes_of(ext[0:targets // 128, :])
     nf[:, 0:targets] = jnp.where(iota((nf.shape[0], targets), 0) == first, 1.0, 0.0).astype(BF16)
 
+    block = 16
+
+    def count_block(b, carry):
+        base = pl.multiple_of(b * block, block)
+        for c0 in range(0, targets, 256):
+            row = iota((block, 256), 0) + base
+            tot = jnp.zeros((block, 256), I32)
+            for k in range(fan_one):
+                tot = tot + jnp.where(row == idx[0, k:k + 1, c0:c0 + 256], idx[1, k:k + 1, c0:c0 + 256], 0)
+            acc[pl.ds(base, block), c0:c0 + 256] = tot
+        return carry
+
+    lax.fori_loop(0, width // block, count_block, 0)
+    for f in range(FIELDS):
+        cnt = lax.bitwise_and(lax.shift_right_logical(acc[...], f * FIELD_BITS), (1 << FIELD_BITS) - 1)
+        nf[f * width:(f + 1) * width, targets:2 * targets] = cnt.astype(F32).astype(BF16)
+
+    for cp in loads[3:]:
+        cp.wait()
+    small[...] = jnp.full(small.shape, -1, I32)
+    small[0:fan_two, 0:seeds] = n2_ref[...]
+    small[12:13, 0:seeds] = lab_ref[...]
+    m2 = jnp.zeros((targets, 128), F32)
+    for k in range(fan_two):
+        m2 = m2 + jnp.where(iota((targets, 128), 0) == small[k:k + 1, :], 1.0, 0.0)
+    m2 = m2.astype(BF16)
+    for src, dst in ((ws1_ref, ws1_t), (wn1_ref, wn1_t), (ws2_ref, ws2_t), (wn2_ref, wn2_t)):
+        dst[...] = src[...].T
+
+    pl.when(first_of_plane)(ask_neighbours)
+
     for cp in asks:
         cp.wait_recv()
     lane = iota((1, 128), 1)
@@ -159,35 +204,7 @@
         reps.append(pltpu.make_async_remote_copy(rep.at[i], rep_in.at[i], hsend.at[2 + i], hrecv.at[2 + i], device_id=(nb,), device_id_type=MESH))
         reps[-1].start()
 
-    block = 16
-
-    def count_block(b, carry):
-        base = pl.multiple_of(b * block, block)
-        for c0 in range(0, targets, 256):
-            row = iota((block, 256), 0) + base
-            tot = jnp.zeros((block, 256), I32)
-            for k in range(fan_one):
-                tot = tot + jnp.where(row == idx[0, k:k + 1, c0:c0 + 256], idx[1, k:k + 1, c0:c0 + 256], 0)
-            acc[pl.ds(base, block), c0:c0 + 256] = tot
-        return carry
-
-    lax.fori_loop(0, width // block, count_block, 0)
-    for f in range(FIELDS):
-        cnt = lax.bitwise_and(lax.shift_right_logical(acc[...], f * FIELD_BITS), (1 << FIELD_BITS) - 1)
-        nf[f * width:(f + 1) * width, targets:2 * targets] = cnt.astype(F32).astype(BF16)
     both[...] = dot(x_ref[...], nf[0:store, :])
-
-    for cp in loads[3:]:
-        cp.wait()
-    small[...] = jnp.full(small.shape, -1, I32)
-    small[0:fan_two, 0:seeds] = n2_ref[...]
-    small[12:13, 0:seeds] = lab_ref[...]
-    m2 = jnp.zeros((targets, 128), F32)
-    for k in range(fan_two):
-        m2 = m2 + jnp.where(iota((targets, 128), 0) == small[k:k + 1, :], 1.0, 0.0)
-    m2 = m2.astype(BF16)
-    for src, dst in ((ws1_ref, ws1_t), (wn1_ref, wn1_t), (ws2_ref, ws2_t), (wn2_ref, wn2_t)):
-        dst[...] = src[...].T
 
     for cp in reps:
         cp.wait_recv()
@@ -285,6 +302,8 @@
             cp.wait_recv()
             tot = tot + parts[w][11][e]
         zc[at:at + n] = tot
+    for d in range(1, nz):
+        pl.when(mz + d < nz)(functools.partial(pl.semaphore_wait, up.at[d], 1))
     quarter = lax.rem(mz, nq)
     in_z = [put(zc.at[pl.ds((zn * lax.rem(zs[d], nq)) // nq, zsize)], lz.at[mz], zdev[d]) for d in range(1, nz)]
     lz[mz] = zc[pl.ds((zn * quarter) // nq, zsize)]
@@ -294,10 +313,15 @@
     for z in range(1, nz):
         tot = tot + lz[z]
     zg[quarter] = tot
+    done = 0
     if nq == 4:
         far = lax.rem(mz + 2 + 4 * lax.rem(mz, 2), nz)
         targets_z = (zdev[1], zdev[nz - 1], dev(far, my, mx, core))
+        done = list(copies) + asks + reps
         in_z = [put(zg.at[quarter], zg.at[quarter], to) for to in targets_z]
+        for cp in done:
+            cp.wait_send()
+        done = len(copies) - 3
         for cp in in_z:
             cp.wait_recv()
     base = [mine + p[4] + p[1][0] * p[3] for p in parts]
@@ -307,37 +331,39 @@
         end = (zn * (q + 1)) // nq
         for t in range(lo, end):
             at = spots[0] + t if t < ca else spots[1] + (t - ca)
-            full[pl.ds(at, 1)] = zg[q, t - lo:t - lo + 1]
+            r_ref[pl.ds(at, 1)] = zg[q, t - lo:t - lo + 1]
     back = []
 
     def spread(w, at):
         n1, _, to, _, _, _, _, _, c, _, _, _ = parts[w]
-        got = [put(full.at[pl.ds(at, c)], full.at[pl.ds(at, c)], to[d]) for d in range(1, n1)]
-        back.append(put(full.at[pl.ds(at, c)], full.at[pl.ds(at, c)], mate))
+        got = [put(r_ref.at[pl.ds(at, c)], r_ref.at[pl.ds(at, c)], to[d]) for d in range(1, n1)]
+        back.append(put(r_ref.at[pl.ds(at, c)], r_ref.at[pl.ds(at, c)], mate))
         return got
 
     second_in = [[], []]
     for w, p in enumerate(parts):
         for e in range(1, p[5]):
-            second_in[w].append(put(full.at[pl.ds(spots[w], p[8])], full.at[pl.ds(spots[w], p[8])], p[7][e]))
+            second_in[w].append(put(r_ref.at[pl.ds(spots[w], p[8])], r_ref.at[pl.ds(spots[w], p[8])], p[7][e]))
     first_in = [[spread(w, spots[w])] for w in range(2)]
     for i in range(max(nx, ny)):
         for w, (n1, own, _, n, off, n2, sub, _, c, _, _, _) in enumerate(parts):
             if i < n2 - 1:
                 second_in[w][i].wait_recv()
                 first_in[w].append(spread(w, base[w] + sub[n2 - 1 - i] * c))
+    for cp in copies[done:] + ([] if done else asks + reps):
+        cp.wait_send()
+    sent = len(copies)
     for i in range(max(nx, ny)):
         for w, (n1, own, _, n, off, n2, sub, _, c, _, _, _) in enumerate(parts):
             if i < n2:
                 for d in range(1, n1):
                     first_in[w][i][d - 1].wait_recv()
                     at = mine + off + own[n1 - d] * n + sub[(n2 - i) % n2] * c
-                    back.append(put(full.at[pl.ds(at, c)], full.at[pl.ds(at, c)], mate))
+                    back.append(put(r_ref.at[pl.ds(at, c)], r_ref.at[pl.ds(at, c)], mate))
     for cp in back:
         cp.wait_recv()
-    for cp in copies + asks + reps:
+    for cp in copies[sent:]:
         cp.wait_send()
-    r_ref[...] = full[...]
 
 
 def copy_count(group):
@@ -408,11 +434,12 @@
                 VMEM((hidden, feat), BF16), VMEM((hidden, feat), BF16), VMEM((hidden, classes), BF16), VMEM((hidden, classes), BF16),
                 VMEM((8, 128), I32), VMEM((2, 8, 128), I32), VMEM((2, frows // 2, 128), BF16),
                 VMEM((2, frows // 2, 128), BF16), dma((4,)), dma((4,)),
+                pltpu.SemaphoreType.REGULAR((nz,)),
                 VMEM((16, 128), I32), VMEM((2, -(-fan_one // 8) * 8, targets), I32), VMEM((width, targets), I32),
                 VMEM((FIELDS * width, 2 * targets), BF16), VMEM((feat, 2 * targets), F32), VMEM((hidden, targets), F32),
                 VMEM((-(-classes // 16) * 16, 128), F32), buf(total),
                 buf(half), buf(half), buf(nx - 1, ny, ca), buf(ny - 1, nx, cb), buf(ny - 1, ca), buf(nx - 1, cb),
-                buf(ny - 1, ca), buf(nx - 1, cb), buf(zn), buf(nz, zsize), buf(nq, zsize), buf(total),
+                buf(ny - 1, ca), buf(nx - 1, cb), buf(zn), buf(nz, zsize), buf(nq, zsize),
                 dma((n,)), dma((n,))],
             compiler_params=pltpu.CompilerParams(collective_id=0, has_side_effects=True,
                                                  vmem_limit_bytes=60 * 1024 * 1024),

time: 58.9 us -> 58.2 us (0.988)
  Pallas kernels: 58.1 us -> 57.4 us
    pallas_call x1, Pallas kernels: 56.5 us -> 55.8 us  [device_step(): pl.pallas_call(functools.partial(step_kernel, group, scale), name='train_...]
where the time goes in v5:
time: 58.2 us; the launch traced here: 58.1 us
  Pallas kernels  57.4 us (99%)
  between operations  0.64 us (1%)
    pallas_call x1, Pallas kernels, device_step(): pl.pallas_call(functools.partial(step_kernel, group, scale), name='train_...  55.8 us
    pallas_call x1, Pallas kernels, device_step(): pl.pallas_call(functools.partial(output_kernel, scale), name='split_outpu...  1.66 us

profile of v5, /device:TPU:1, one launch (start us, length us, event | category | flops | bytes accessed | tf_op | source)
XLA Modules:
  0.0 58.1 jit_solution(7159008998298851789)
XLA Ops:
  0.6 55.8 %train_step.1.r_ref = f32[352,8,128]{2,1,0:T(8,128)S(1)} custom-call(s32[16,128]{1,0:T(8,128)} %bitcast.14, bf16[602,2048]{1,0:T(8,128)(2,1)} %bitcast.10, s32[25,512]{1,0:T(8,128)} %bitcast.11, s32[10,64]{1,0:T(8,128)} %bitcast.15, s32[1,64]{1,0:T(1,128)} %bitcast.16, bf16[602,256]{1,0:T(8,128)(2,1)} %ws1_hbm.1, bf16[602,256]{1,0:T(8,128)(2,1)} %wn1_hbm.1, ...), custom_call_target="tpu_custom_call" | custom-call | tf_op jit(solution)/shard_map/train_step/pallas_call | solution.py:424
  56.4 1.7 %split_outputs.1 = (f32[1,1]{1,0:T(1,128)}, f32[602,256]{1,0:T(8,128)}, f32[602,256]{1,0:T(8,128)}, f32[41,256]{1,0:T(8,128)}, f32[41,256]{1,0:T(8,128)}) custom-call(f32[352,8,128]{2,1,0:T(8,128)S(1)} %train_step.1.r_ref), custom_call_target="tpu_custom_call" | custom-call | tf_op jit(solution)/shard_map/split_outputs/pallas_call | solution.py:447

commit v6 on v5

--- a/solution.py
+++ b/solution.py
@@ -29,6 +29,10 @@
 
 def iota(shape, dim):
     return lax.broadcasted_iota(I32, shape, dim)
+
+
+def far_first(n):
+    return sorted(range(1, n), key=lambda d: -min(d, n - d)) + [0]
 
 
 def frontier_ext(fid, me, group, rows_log2):
@@ -270,7 +274,7 @@
     for i in range(max(nx, ny)):
         for w, p in enumerate(parts):
             if i < p[0]:
-                d = (i + 1) % p[0]
+                d = far_first(p[0])[i]
                 pieces.append((w, d, p[4] + p[1][d] * p[3]))
     arrive = [put(g.at[pl.ds(other + o, parts[w][3])], rc.at[pl.ds(o, parts[w][3])], mate) for w, d, o in pieces]
     first_in = [{}, {}]
@@ -280,32 +284,32 @@
         part[pl.ds(o, n)] = g[pl.ds(mine + o, n)] + rc[pl.ds(o, n)]
         if d:
             for i in range(n2):
-                e = (i + 1) % n2
+                e = far_first(n2)[i]
                 first_in[w][d, e] = put(part.at[pl.ds(o + sub[e] * c, c)], land.at[d - 1, e], to[d])
     second_in, sums = [[], []], [None, None]
     for i in range(max(nx, ny)):
         for w, (n1, own, _, n, off, n2, sub, to, c, land, w2, l2) in enumerate(parts):
             if i < n2:
-                e = (i + 1) % n2
+                e = far_first(n2)[i]
                 tot = part[pl.ds(off + own[0] * n + sub[e] * c, c)]
                 for d in range(1, n1):
                     first_in[w][d, e].wait_recv()
                     tot = tot + land[d - 1, e]
                 if e:
                     w2[e - 1] = tot
-                    second_in[w].append(put(w2.at[e - 1], l2.at[e - 1], to[e]))
+                    second_in[w].append((e, put(w2.at[e - 1], l2.at[e - 1], to[e])))
                 else:
                     sums[w] = tot
     for w, at, n in ((0, 0, ca), (1, ca, cb)):
         tot = sums[w]
-        for e, cp in enumerate(second_in[w]):
+        for e, cp in second_in[w]:
             cp.wait_recv()
-            tot = tot + parts[w][11][e]
+            tot = tot + parts[w][11][e - 1]
         zc[at:at + n] = tot
     for d in range(1, nz):
         pl.when(mz + d < nz)(functools.partial(pl.semaphore_wait, up.at[d], 1))
     quarter = lax.rem(mz, nq)
-    in_z = [put(zc.at[pl.ds((zn * lax.rem(zs[d], nq)) // nq, zsize)], lz.at[mz], zdev[d]) for d in range(1, nz)]
+    in_z = [put(zc.at[pl.ds((zn * lax.rem(zs[d], nq)) // nq, zsize)], lz.at[mz], zdev[d]) for d in far_first(nz)[:-1]]
     lz[mz] = zc[pl.ds((zn * quarter) // nq, zsize)]
     for cp in in_z:
         cp.wait_recv()
@@ -316,7 +320,7 @@
     done = 0
     if nq == 4:
         far = lax.rem(mz + 2 + 4 * lax.rem(mz, 2), nz)
-        targets_z = (zdev[1], zdev[nz - 1], dev(far, my, mx, core))
+        targets_z = (dev(far, my, mx, core), zdev[1], zdev[nz - 1])
         done = list(copies) + asks + reps
         in_z = [put(zg.at[quarter], zg.at[quarter], to) for to in targets_z]
         for cp in done:
@@ -336,29 +340,31 @@
 
     def spread(w, at):
         n1, _, to, _, _, _, _, _, c, _, _, _ = parts[w]
-        got = [put(r_ref.at[pl.ds(at, c)], r_ref.at[pl.ds(at, c)], to[d]) for d in range(1, n1)]
+        got = {d: put(r_ref.at[pl.ds(at, c)], r_ref.at[pl.ds(at, c)], to[d]) for d in far_first(n1)[:-1]}
         back.append(put(r_ref.at[pl.ds(at, c)], r_ref.at[pl.ds(at, c)], mate))
         return got
 
-    second_in = [[], []]
+    second_in = [{}, {}]
     for w, p in enumerate(parts):
-        for e in range(1, p[5]):
-            second_in[w].append(put(r_ref.at[pl.ds(spots[w], p[8])], r_ref.at[pl.ds(spots[w], p[8])], p[7][e]))
+        for e in far_first(p[5])[:-1]:
+            second_in[w][e] = (put(r_ref.at[pl.ds(spots[w], p[8])], r_ref.at[pl.ds(spots[w], p[8])], p[7][e]))
     first_in = [[spread(w, spots[w])] for w in range(2)]
     for i in range(max(nx, ny)):
         for w, (n1, own, _, n, off, n2, sub, _, c, _, _, _) in enumerate(parts):
             if i < n2 - 1:
-                second_in[w][i].wait_recv()
-                first_in[w].append(spread(w, base[w] + sub[n2 - 1 - i] * c))
+                e = far_first(n2)[n2 - 2 - i]
+                second_in[w][e].wait_recv()
+                first_in[w].append(spread(w, base[w] + sub[n2 - e] * c))
     for cp in copies[done:] + ([] if done else asks + reps):
         cp.wait_send()
     sent = len(copies)
     for i in range(max(nx, ny)):
         for w, (n1, own, _, n, off, n2, sub, _, c, _, _, _) in enumerate(parts):
             if i < n2:
-                for d in range(1, n1):
-                    first_in[w][i][d - 1].wait_recv()
-                    at = mine + off + own[n1 - d] * n + sub[(n2 - i) % n2] * c
+                e = far_first(n2)[n2 - 1 - i]
+                for d in reversed(far_first(n1)[:-1]):
+                    first_in[w][i][d].wait_recv()
+                    at = mine + off + own[n1 - d] * n + sub[(n2 - e) % n2] * c
                     back.append(put(r_ref.at[pl.ds(at, c)], r_ref.at[pl.ds(at, c)], mate))
     for cp in back:
         cp.wait_recv()

time: 58.2 us -> 56.3 us (0.967)
  Pallas kernels: 57.4 us -> 55.5 us
    pallas_call x1, Pallas kernels: 55.8 us -> 53.8 us  [device_step(): pl.pallas_call(functools.partial(step_kernel, group, scale), name='train_...]
where the time goes in v6:
time: 56.3 us; the launch traced here: 56.1 us
  Pallas kernels  55.5 us (99%)
  between operations  0.64 us (1%)
    pallas_call x1, Pallas kernels, device_step(): pl.pallas_call(functools.partial(step_kernel, group, scale), name='train_...  53.8 us
    pallas_call x1, Pallas kernels, device_step(): pl.pallas_call(functools.partial(output_kernel, scale), name='split_outpu...  1.66 us

profile of v6, /device:TPU:1, one launch (start us, length us, event | category | flops | bytes accessed | tf_op | source)
XLA Modules:
  0.0 56.1 jit_solution(13278933855285741949)
XLA Ops:
  0.6 53.8 %train_step.1.r_ref = f32[352,8,128]{2,1,0:T(8,128)S(1)} custom-call(s32[16,128]{1,0:T(8,128)} %bitcast.14, bf16[602,2048]{1,0:T(8,128)(2,1)} %bitcast.10, s32[25,512]{1,0:T(8,128)} %bitcast.11, s32[10,64]{1,0:T(8,128)} %bitcast.15, s32[1,64]{1,0:T(1,128)} %bitcast.16, bf16[602,256]{1,0:T(8,128)(2,1)} %ws1_hbm.1, bf16[602,256]{1,0:T(8,128)(2,1)} %wn1_hbm.1, ...), custom_call_target="tpu_custom_call" | custom-call | tf_op jit(solution)/shard_map/train_step/pallas_call | solution.py:430
  54.5 1.7 %split_outputs.1 = (f32[1,1]{1,0:T(1,128)}, f32[602,256]{1,0:T(8,128)}, f32[602,256]{1,0:T(8,128)}, f32[41,256]{1,0:T(8,128)}, f32[41,256]{1,0:T(8,128)}) custom-call(f32[352,8,128]{2,1,0:T(8,128)S(1)} %train_step.1.r_ref), custom_call_target="tpu_custom_call" | custom-call | tf_op jit(solution)/shard_map/split_outputs/pallas_call | solution.py:453

commit v7 on v6

--- a/solution.py
+++ b/solution.py
@@ -197,24 +197,32 @@
     want = jnp.where(lane < HALO, ask_in[0, 0:1, :], ask_in[1, 0:1, :])
     pick = jnp.where(iota((store, 128), 0) == want, 1.0, 0.0).astype(BF16)
     loads[2].wait()
-    out = dot(x_ref[...], pick)
-    top = out[0:hrows]
-    bot = jnp.concatenate([out[hrows:feat], jnp.zeros((2 * hrows - feat, 128), F32)], axis=0)
-    low = iota((hrows, 128), 1) < HALO
-    rep[0] = jnp.where(low, top, pltpu.roll(bot, HALO, 1)).astype(BF16)
-    rep[1] = jnp.where(low, pltpu.roll(top, HALO, 1), bot).astype(BF16)
     reps = []
-    for i, nb in enumerate((right, left)):
-        reps.append(pltpu.make_async_remote_copy(rep.at[i], rep_in.at[i], hsend.at[2 + i], hrecv.at[2 + i], device_id=(nb,), device_id_type=MESH))
-        reps[-1].start()
+    cut = 16 * (hrows // 32 + 1)
+    for i, (lo, n) in enumerate(((0, cut), (cut, hrows - cut))):
+        out = dot(x_ref[2 * lo:min(2 * lo + 2 * n, feat), :], pick)
+        if out.shape[0] < 2 * n:
+            out = jnp.concatenate([out, jnp.zeros((2 * n - out.shape[0], 128), F32)], axis=0)
+        top, bot = out[0:n], out[n:2 * n]
+        low = iota((n, 128), 1) < HALO
+        rep[0, lo:lo + n] = jnp.where(low, top, pltpu.roll(bot, HALO, 1)).astype(BF16)
+        rep[1, lo:lo + n] = jnp.where(low, pltpu.roll(top, HALO, 1), bot).astype(BF16)
+        for k, nb in enumerate((right, left)):
+            reps.append(pltpu.make_async_remote_copy(rep.at[k, lo:lo + n], rep_in.at[k, lo:lo + n], hsend.at[2 + 2 * i + k],
+                                                     hrecv.at[2 + 2 * i + k], device_id=(nb,), device_id_type=MESH))
+            reps[-1].start()
 
     both[...] = dot(x_ref[...], nf[0:store, :])
 
     for cp in reps:
         cp.wait_recv()
-    from_l, from_r = rep_in[0].astype(F32), rep_in[1].astype(F32)
-    halo = jnp.concatenate([jnp.where(low, from_l, pltpu.roll(from_r, HALO, 1)).astype(BF16),
-                            jnp.where(low, pltpu.roll(from_l, HALO, 1), from_r).astype(BF16)], axis=0)
+    halves = []
+    for lo, n in ((0, cut), (cut, hrows - cut)):
+        low = iota((n, 128), 1) < HALO
+        from_l, from_r = rep_in[0, lo:lo + n].astype(F32), rep_in[1, lo:lo + n].astype(F32)
+        halves += [jnp.where(low, from_l, pltpu.roll(from_r, HALO, 1)).astype(BF16),
+                   jnp.where(low, pltpu.roll(from_l, HALO, 1), from_r).astype(BF16)]
+    halo = jnp.concatenate(halves, axis=0)
     rows = both[...] + dot(halo[0:feat], nf[store:store + 2 * HALO, :])
     x_t = rows[:, 0:targets].astype(BF16)
     a_t = (rows[:, targets:] * (1.0 / fan_one)).astype(BF16)
@@ -439,7 +447,7 @@
                 VMEM((classes, hidden), BF16), dma((9,)),
                 VMEM((hidden, feat), BF16), VMEM((hidden, feat), BF16), VMEM((hidden, classes), BF16), VMEM((hidden, classes), BF16),
                 VMEM((8, 128), I32), VMEM((2, 8, 128), I32), VMEM((2, frows // 2, 128), BF16),
-                VMEM((2, frows // 2, 128), BF16), dma((4,)), dma((4,)),
+                VMEM((2, frows // 2, 128), BF16), dma((6,)), dma((6,)),
                 pltpu.SemaphoreType.REGULAR((nz,)),
                 VMEM((16, 128), I32), VMEM((2, -(-fan_one // 8) * 8, targets), I32), VMEM((width, targets), I32),
                 VMEM((FIELDS * width, 2 * targets), BF16), VMEM((feat, 2 * targets), F32), VMEM((hidden, targets), F32),

time: 56.3 us -> 55.7 us (0.989)
  Pallas kernels: 55.5 us -> 54.9 us
    pallas_call x1, Pallas kernels: 53.8 us -> 53.3 us  [device_step(): pl.pallas_call(functools.partial(step_kernel, group, scale), name='train_...]
where the time goes in v7:
time: 55.7 us; the launch traced here: 55.6 us
  Pallas kernels  54.9 us (99%)
  between operations  0.64 us (1%)
    pallas_call x1, Pallas kernels, device_step(): pl.pallas_call(functools.partial(step_kernel, group, scale), name='train_...  53.3 us
    pallas_call x1, Pallas kernels, device_step(): pl.pallas_call(functools.partial(output_kernel, scale), name='split_outpu...  1.66 us

profile of v7, /device:TPU:1, one launch (start us, length us, event | category | flops | bytes accessed | tf_op | source)
XLA Modules:
  0.0 55.6 jit_solution(5501454003210131591)
XLA Ops:
  0.6 53.3 %train_step.1.r_ref = f32[352,8,128]{2,1,0:T(8,128)S(1)} custom-call(s32[16,128]{1,0:T(8,128)} %bitcast.14, bf16[602,2048]{1,0:T(8,128)(2,1)} %bitcast.10, s32[25,512]{1,0:T(8,128)} %bitcast.11, s32[10,64]{1,0:T(8,128)} %bitcast.15, s32[1,64]{1,0:T(1,128)} %bitcast.16, bf16[602,256]{1,0:T(8,128)(2,1)} %ws1_hbm.1, bf16[602,256]{1,0:T(8,128)(2,1)} %wn1_hbm.1, ...), custom_call_target="tpu_custom_call" | custom-call | tf_op jit(solution)/shard_map/train_step/pallas_call | solution.py:438
  53.9 1.7 %split_outputs.1 = (f32[1,1]{1,0:T(1,128)}, f32[602,256]{1,0:T(8,128)}, f32[602,256]{1,0:T(8,128)}, f32[41,256]{1,0:T(8,128)}, f32[41,256]{1,0:T(8,128)}) custom-call(f32[352,8,128]{2,1,0:T(8,128)S(1)} %train_step.1.r_ref), custom_call_target="tpu_custom_call" | custom-call | tf_op jit(solution)/shard_map/split_outputs/pallas_call | solution.py:461

commit v8 on v7

--- a/solution.py
+++ b/solution.py
@@ -198,8 +198,8 @@
     pick = jnp.where(iota((store, 128), 0) == want, 1.0, 0.0).astype(BF16)
     loads[2].wait()
     reps = []
-    cut = 16 * (hrows // 32 + 1)
-    for i, (lo, n) in enumerate(((0, cut), (cut, hrows - cut))):
+    cuts = [(0, 112), (112, 96), (208, hrows - 208)]
+    for i, (lo, n) in enumerate(cuts):
         out = dot(x_ref[2 * lo:min(2 * lo + 2 * n, feat), :], pick)
         if out.shape[0] < 2 * n:
             out = jnp.concatenate([out, jnp.zeros((2 * n - out.shape[0], 128), F32)], axis=0)
@@ -217,7 +217,7 @@
     for cp in reps:
         cp.wait_recv()
     halves = []
-    for lo, n in ((0, cut), (cut, hrows - cut)):
+    for lo, n in cuts:
         low = iota((n, 128), 1) < HALO
         from_l, from_r = rep_in[0, lo:lo + n].astype(F32), rep_in[1, lo:lo + n].astype(F32)
         halves += [jnp.where(low, from_l, pltpu.roll(from_r, HALO, 1)).astype(BF16),
@@ -447,7 +447,7 @@
                 VMEM((classes, hidden), BF16), dma((9,)),
                 VMEM((hidden, feat), BF16), VMEM((hidden, feat), BF16), VMEM((hidden, classes), BF16), VMEM((hidden, classes), BF16),
                 VMEM((8, 128), I32), VMEM((2, 8, 128), I32), VMEM((2, frows // 2, 128), BF16),
-                VMEM((2, frows // 2, 128), BF16), dma((6,)), dma((6,)),
+                VMEM((2, frows // 2, 128), BF16), dma((8,)), dma((8,)),
                 pltpu.SemaphoreType.REGULAR((nz,)),
                 VMEM((16, 128), I32), VMEM((2, -(-fan_one // 8) * 8, targets), I32), VMEM((width, targets), I32),
                 VMEM((FIELDS * width, 2 * targets), BF16), VMEM((feat, 2 * targets), F32), VMEM((hidden, targets), F32),

time: 55.7 us -> 55.4 us (level)
  no operation moved by 1% of the time
where the time goes in v8:
time: 55.4 us; the launch traced here: 55.2 us
  Pallas kernels  54.6 us (99%)
  between operations  0.64 us (1%)
    pallas_call x1, Pallas kernels, device_step(): pl.pallas_call(functools.partial(step_kernel, group, scale), name='train_...  52.9 us
    pallas_call x1, Pallas kernels, device_step(): pl.pallas_call(functools.partial(output_kernel, scale), name='split_outpu...  1.66 us

profile of v8, /device:TPU:1, one launch (start us, length us, event | category | flops | bytes accessed | tf_op | source)
XLA Modules:
  0.0 55.2 jit_solution(7975045415940613449)
XLA Ops:
  0.6 52.9 %train_step.1.r_ref = f32[352,8,128]{2,1,0:T(8,128)S(1)} custom-call(s32[16,128]{1,0:T(8,128)} %bitcast.14, bf16[602,2048]{1,0:T(8,128)(2,1)} %bitcast.10, s32[25,512]{1,0:T(8,128)} %bitcast.11, s32[10,64]{1,0:T(8,128)} %bitcast.15, s32[1,64]{1,0:T(1,128)} %bitcast.16, bf16[602,256]{1,0:T(8,128)(2,1)} %ws1_hbm.1, bf16[602,256]{1,0:T(8,128)(2,1)} %wn1_hbm.1, ...), custom_call_target="tpu_custom_call" | custom-call | tf_op jit(solution)/shard_map/train_step/pallas_call | solution.py:438
  53.6 1.7 %split_outputs.1 = (f32[1,1]{1,0:T(1,128)}, f32[602,256]{1,0:T(8,128)}, f32[602,256]{1,0:T(8,128)}, f32[41,256]{1,0:T(8,128)}, f32[41,256]{1,0:T(8,128)}) custom-call(f32[352,8,128]{2,1,0:T(8,128)S(1)} %train_step.1.r_ref), custom_call_target="tpu_custom_call" | custom-call | tf_op jit(solution)/shard_map/split_outputs/pallas_call | solution.py:461
